TPU v7x, 768 devices: a whole 4x8x12 slice. The times are simulated.
768 devices in a mesh: slab: 768 (over y, z, x, core).
Axes of the slice: x: 4, y: 8, z: 12, core: 2. Of those that a mesh axis runs over, the one named last changes fastest.
Arguments:
- load_terms: float32 [8, 8, 8, 98304], P(None, None, None, 'slab'), may hold values from -12 to 12
- geometry: float32 [3, 8, 8, 8, 98304], P(None, None, None, None, 'slab'), may hold values from 0.02 to 0.2
- mass_terms: float32 [8, 8, 8, 98304], P(None, None, None, 'slab'), may hold values from 1 to 4
- element_order: int32 [768, 128], P('slab'), may hold values from 0 to 127, each once within a row
Outputs:
- solution: float32 [8, 8, 8, 98304], P(None, None, None, 'slab')
- residual: float32 [8, 8, 8, 98304], P(None, None, None, 'slab')
Inputs may be any that keep to these rules, and one draw needn't show every extreme that they name: `element_order`: each device's row lists each of its 128 cells once.
All inputs are finite; a program needn't handle non-finite values.
Results may differ from a plain program's by a relative error of at most 0.0001.
Values sent between devices are 32-bit elements; how exact they have to be, the bound alone decides.
No kernel may reach another device: no remote copies, remote signals or barrier semaphores. Data moves between devices by JAX's collectives and lax.ppermute only.
A program may use at most 32 MiB of HBM per device.

v0:
```python
import functools

import jax
import jax.numpy as jnp
import numpy as np
from jax import lax
from jax.sharding import Mesh
from jax.sharding import PartitionSpec as P

EL_X = 1
EL_Y = 8
EL_Z = 16
SLAB = ("slab_0", "slab_1", "slab_2", "slab_3")


spectrum_centre = 1.65
spectrum_half = 1.35


def padded_2(block, sides, width):
    for axis, dim in sides:
        count = lax.axis_size(axis)
        forward = [(i, i + 1) for i in range(count - 1)]
        forward.append((count - 1, 0))
        backward = [(target, source) for source, target in forward]
        low = lax.ppermute(
            lax.slice_in_dim(block, block.shape[dim] - width, None, axis=dim), axis, forward
        )
        high = lax.ppermute(lax.slice_in_dim(block, 0, width, axis=dim), axis, backward)
        block = jnp.concatenate([low, block, high], axis=dim)
    return block


def over_axes(shard, axes):
    return functools.reduce(lax.psum, axes, shard)


def legendre_table(positions, points):
    columns = [positions * 0.0 + 1.0, positions]
    for degree_now in range(2, points):
        columns.append(
            ((2 * degree_now - 1) * positions * columns[-1] - (degree_now - 1) * columns[-2])
            / degree_now
        )
    return np.stack(columns, axis=1)


def gll_derivative(points):
    degree = points - 1
    grid_nodes = -np.cos(np.pi * np.arange(points) / degree)
    for repeat in range(100):
        legendre = legendre_table(grid_nodes, points)
        grid_nodes = grid_nodes - (grid_nodes * legendre[:, degree] - legendre[:, degree - 1]) / (
            points * legendre[:, degree]
        )
    legendre = legendre_table(grid_nodes, points)
    top_values = legendre[:, degree]
    index_list = np.arange(points)
    same_index = index_list[:, None] == index_list[None, :]
    spacing = grid_nodes[:, None] - grid_nodes[None, :]
    spacing = np.where(same_index, 1.0, spacing)
    deriv_table = top_values[:, None] / (top_values[None, :] * spacing)
    deriv_table = np.where(same_index, 0.0, deriv_table)
    deriv_table[0, 0] = -degree * points / 4.0
    deriv_table[degree, degree] = degree * points / 4.0
    return deriv_table


def local_apply(values, geometry, mass_terms, deriv_table):
    highest = lax.Precision.HIGHEST
    grad_one = jnp.einsum("ma,abce->mbce", deriv_table, values, precision=highest)
    result = jnp.einsum("ma,mbce->abce", deriv_table, geometry[0] * grad_one, precision=highest)
    grad_two = jnp.einsum("mb,abce->amce", deriv_table, values, precision=highest)
    result = result + jnp.einsum(
        "mb,amce->abce", deriv_table, geometry[1] * grad_two, precision=highest
    )
    grad_three = jnp.einsum("mc,abce->abme", deriv_table, values, precision=highest)
    result = result + jnp.einsum(
        "mc,abme->abce", deriv_table, geometry[2] * grad_three, precision=highest
    )
    return result + mass_terms * values


def local_diagonal(geometry, mass_terms, deriv_table):
    highest = lax.Precision.HIGHEST
    squared = deriv_table * deriv_table
    result = jnp.einsum("ma,mbce->abce", squared, geometry[0], precision=highest)
    result = result + jnp.einsum("mb,amce->abce", squared, geometry[1], precision=highest)
    result = result + jnp.einsum("mc,abme->abce", squared, geometry[2], precision=highest)
    return result + mass_terms


def build_tables(element_order):
    cell_ids = element_order[0]
    elem_count = cell_ids.shape[0]
    cross_count = EL_Y * EL_Z
    column_ids = jnp.arange(elem_count, dtype=jnp.int32)
    inverse = jnp.zeros((elem_count,), jnp.int32).at[cell_ids].set(column_ids)
    pos_x = cell_ids // cross_count
    pos_y = cell_ids // EL_Z % EL_Y
    pos_z = cell_ids % EL_Z
    across = pos_y * EL_Z + pos_z
    plus_x = jnp.where(
        pos_x + 1 < EL_X,
        inverse[jnp.minimum(cell_ids + cross_count, elem_count - 1)],
        elem_count + across,
    )
    minus_x = jnp.where(
        pos_x > 0, inverse[jnp.maximum(cell_ids - cross_count, 0)], elem_count + across
    )
    plus_y = jnp.where(
        pos_y + 1 < EL_Y, inverse[jnp.minimum(cell_ids + EL_Z, elem_count - 1)], elem_count
    )
    minus_y = jnp.where(pos_y > 0, inverse[jnp.maximum(cell_ids - EL_Z, 0)], elem_count)
    base_z = cell_ids - pos_z
    plus_z = inverse[base_z + (pos_z + 1) % EL_Z]
    minus_z = inverse[base_z + (pos_z + EL_Z - 1) % EL_Z]
    return {
        "plus_x": plus_x,
        "minus_x": minus_x,
        "plus_y": plus_y,
        "minus_y": minus_y,
        "plus_z": plus_z,
        "minus_z": minus_z,
        "pos_y": pos_y,
        "first_cols": inverse,
        "last_cols": inverse,
    }


def node_weights(tables, points):
    node_ids = jnp.arange(points)
    end_node = (node_ids == 0) | (node_ids == points - 1)
    edge_mult = jnp.where(end_node, 2.0, 1.0).astype(jnp.float32)
    pos_y = tables["pos_y"]
    low_shared = (node_ids == 0)[:, None] & (pos_y > 0)[None, :]
    high_shared = (node_ids == points - 1)[:, None] & (pos_y < EL_Y - 1)[None, :]
    mid_mult = jnp.where(low_shared | high_shared, 2.0, 1.0).astype(jnp.float32)
    return 1.0 / (
        edge_mult[:, None, None, None] * mid_mult[None, :, None, :] * edge_mult[None, None, :, None]
    )


def boundary_faces(values, tables):
    low_face = jnp.take(values[0], tables["first_cols"], axis=2)
    high_face = jnp.take(values[-1], tables["last_cols"], axis=2)
    return jnp.stack([low_face, high_face])


def assemble(values, tables, padded):
    low_face = values[0]
    high_face = values[-1]
    low_ext = jnp.concatenate([low_face, padded[3]], axis=2)
    high_ext = jnp.concatenate([high_face, padded[0]], axis=2)
    new_high = high_face + jnp.take(low_ext, tables["plus_x"], axis=2)
    new_low = low_face + jnp.take(high_ext, tables["minus_x"], axis=2)
    values = jnp.concatenate([new_low[None], values[1:-1], new_high[None]], axis=0)
    low_face = values[:, 0]
    high_face = values[:, -1]
    zero_column = jnp.zeros(low_face.shape[:2] + (1,), values.dtype)
    low_ext = jnp.concatenate([low_face, zero_column], axis=2)
    high_ext = jnp.concatenate([high_face, zero_column], axis=2)
    new_high = high_face + jnp.take(low_ext, tables["plus_y"], axis=2)
    new_low = low_face + jnp.take(high_ext, tables["minus_y"], axis=2)
    values = jnp.concatenate([new_low[:, None], values[:, 1:-1], new_high[:, None]], axis=1)
    low_face = values[:, :, 0]
    high_face = values[:, :, -1]
    new_high = high_face + jnp.take(low_face, tables["plus_z"], axis=2)
    new_low = low_face + jnp.take(high_face, tables["minus_z"], axis=2)
    return jnp.concatenate([new_low[:, :, None], values[:, :, 1:-1], new_high[:, :, None]], axis=2)


def on_device(load_terms, geometry, mass_terms, element_order):
    points = load_terms.shape[0]
    deriv_table = jnp.asarray(gll_derivative(points), jnp.float32)
    tables = build_tables(element_order)
    weight = node_weights(tables, points)
    diag_local = local_diagonal(geometry, mass_terms, deriv_table)
    stacked = jnp.stack([boundary_faces(load_terms, tables), boundary_faces(diag_local, tables)])
    both_faces = padded_2(stacked, ((SLAB, 1),), 1)
    load_padded = both_faces[0]
    diag_padded = both_faces[1]
    start = assemble(load_terms, tables, load_padded)
    inv_diag = 1.0 / assemble(diag_local, tables, diag_padded)

    def operate(values):
        local_part = local_apply(values, geometry, mass_terms, deriv_table)
        padded = padded_2(boundary_faces(local_part, tables), ((SLAB, 0),), 1)
        return assemble(local_part, tables, padded)

    ratio_sigma = spectrum_centre / spectrum_half
    step_vec = inv_diag * start / spectrum_centre
    precond = step_vec
    rho_prev = 1.0 / ratio_sigma
    rho_next = 1.0 / (2.0 * ratio_sigma - rho_prev)
    misfit = start - operate(precond)
    step_vec = rho_next * rho_prev * step_vec + 2.0 * rho_next / spectrum_half * inv_diag * misfit
    precond = precond + step_vec
    image_vec = operate(precond)
    numerator, denominator = (
        over_axes(jnp.sum(weight * start * precond), SLAB),
        over_axes(jnp.sum(weight * precond * image_vec), SLAB),
    )
    step_size = numerator / denominator
    return (step_size * precond, start - step_size * image_vec)


def solution(mesh):
    torus = Mesh(mesh.devices.reshape(8, 12, 4, 2), ("slab_0", "slab_1", "slab_2", "slab_3"))
    placed = (
        P(None, None, None, SLAB),
        P(None, None, None, None, SLAB),
        P(None, None, None, SLAB),
        P(SLAB, None),
    )
    return jax.shard_map(
        on_device,
        mesh=torus,
        in_specs=placed,
        out_specs=(P(None, None, None, SLAB), P(None, None, None, SLAB)),
        check_vma=False,
    )
```

profile of v0, /device:TPU:1, one launch (start us, length us, event | category | flops | bytes accessed | tf_op | source)
XLA Modules:
  0.0 235.8 jit_solution(11798250117350814003)
XLA Ops:
  0.6 1.3 fusion.54
  1.9 1.3 fusion.55
  4.2 1.1 fusion.66
  11.7 1.7 gather_fusion.6
  13.6 1.0 copy.50
  14.7 1.7 gather_fusion.7
  17.2 12.4 %collective-permute-start.1 = (f32[2,1,8,8,128]{4,3,2,1,0:T(8,128)S(1)}, f32[2,1,8,8,128]{4,3,2,1,0:T(8,128)S(1)}, u32[]{:S(2)}, u32[]{:S(2)}) collective-permute-start(f32[2,1,8,8,128]{4,3,2,1,0:T(8,128)S(1)} %get-tuple-element.71), channel_id=1, source_target_pairs={{1,0},{2,1},{3,2},{4,3},{5,4},{6,5},{7,6},{8,7},{9,8},{10,9},{11,1... | collective-permute-start | bytes 196616 | tf_op jit(solution)/shard_map/ppermute | solution.py:29
  29.6 1.9 collective-permute-start
  32.2 1.2 gather_fusion.4
  34.7 1.2 gather_fusion.5
  37.3 1.2 gather_fusion.2
  39.0 1.2 gather_fusion.3
  40.3 1.2 gather_fusion
  41.5 1.4 gather_fusion.1
  45.5 1.6 gather_fusion.17
  47.0 1.2 copy.84
  48.2 1.4 slice_bitcast_fusion.7
  50.1 1.6 gather_fusion.16
  51.6 1.2 copy.82
  53.3 1.6 gather_fusion.11
  54.8 1.2 copy.67
  56.5 1.6 gather_fusion.10
  58.1 1.2 copy.64
  66.4 1.0 copy.75
  67.4 2.5 %gather_fusion.14 = f32[128,8,8]{2,1,0:T(8,128)} fusion(f32[8,8,128]{1,0,2:T(8,128)} %copy.75, s32[1024]{0:T(1024)S(1)} %pad_clamp_fusion.2), kind=kCustom, calls=%fused_computation.6.clone | custom fusion | bytes 66048 | tf_op jit(solution)/shard_map/jit(_take)/gather | solution.py:169
  69.9 1.2 copy.76
  71.1 1.0 copy.77
  72.1 2.5 %gather_fusion.15 = f32[128,8,8]{2,1,0:T(8,128)} fusion(f32[8,8,128]{1,0,2:T(8,128)} %copy.77, s32[1024]{0:T(1024)S(1)} %pad_clamp_fusion), kind=kCustom, calls=%fused_computation.7.clone | custom fusion | bytes 66048 | tf_op jit(solution)/shard_map/jit(_take)/gather | solution.py:168
  74.6 1.2 copy.78
  75.8 1.0 copy.95
  76.9 2.5 %gather_fusion.21 = f32[128,8,8]{2,1,0:T(8,128)} fusion(f32[8,8,128]{1,0,2:T(8,128)} %copy.95, s32[1024]{0:T(1024)S(1)} %pad_clamp_fusion), kind=kCustom, calls=%fused_computation.9.clone | custom fusion | bytes 66048 | tf_op jit(solution)/shard_map/jit(_take)/gather | solution.py:168
  79.3 1.2 copy.96
  80.5 1.0 copy.93
  81.6 2.5 %gather_fusion.20 = f32[128,8,8]{2,1,0:T(8,128)} fusion(f32[8,8,128]{1,0,2:T(8,128)} %copy.93, s32[1024]{0:T(1024)S(1)} %pad_clamp_fusion.2), kind=kCustom, calls=%fused_computation.8.clone | custom fusion | bytes 66048 | tf_op jit(solution)/shard_map/jit(_take)/gather | solution.py:169
  84.0 1.2 copy.94
  89.7 2.5 %gather_fusion.24 = f32[128,8,8]{2,1,0:T(8,128)} fusion(f32[8,8,128]{1,0,2:T(8,128)} %copy.105, s32[1024]{0:T(1024)S(1)} %pad_clamp_fusion.11), kind=kCustom, calls=%fused_computation.11.clone | custom fusion | bytes 66048 | tf_op jit(solution)/shard_map/jit(_take)/gather | solution.py:145
  92.2 1.2 copy.106
  93.4 1.0 copy.101
  94.4 2.5 %gather_fusion.22 = f32[128,8,8]{2,1,0:T(8,128)} fusion(f32[8,8,128]{1,0,2:T(8,128)} %copy.101, s32[1024]{0:T(1024)S(1)} %pad_clamp_fusion.11), kind=kCustom, calls=%fused_computation.10.clone | custom fusion | bytes 66048 | tf_op jit(solution)/shard_map/jit(_take)/gather | solution.py:146
  96.9 1.2 copy.102
  98.8 10.1 %collective-permute-start.3 = (f32[1,8,8,128]{3,2,1,0:T(8,128)S(1)}, f32[1,8,8,128]{3,2,1,0:T(8,128)S(1)}, u32[]{:S(2)}, u32[]{:S(2)}) collective-permute-start(f32[1,8,8,128]{3,2,1,0:T(8,128)S(1)} %get-tuple-element.81), channel_id=1, source_target_pairs={{1,0},{2,1},{3,2},{4,3},{5,4},{6,5},{7,6},{8,7},{9,8},{10,9},{11,1... | collective-permute-start | bytes 98312 | tf_op jit(solution)/shard_map/ppermute | solution.py:29
  109.0 2.1 collective-permute-start.2
  111.3 1.4 copy.107
  112.7 2.8 %gather_fusion.25 = f32[128,8,8]{2,1,0:T(8,128)} fusion(f32[8,8,256]{1,0,2:T(8,128)} %copy.107, s32[1024]{0:T(1024)} %copy-done.15), kind=kCustom, calls=%fused_computation.22.clone | custom fusion | bytes 66048 | tf_op jit(solution)/shard_map/jit(_take)/gather | solution.py:155
  115.5 1.2 copy.108
  116.7 2.3 collective-permute-done.2
  119.0 1.4 copy.103
  120.3 2.8 %gather_fusion.23 = f32[128,8,8]{2,1,0:T(8,128)} fusion(f32[8,8,256]{1,0,2:T(8,128)} %copy.103, s32[1024]{0:T(1024)} %copy-done.14), kind=kCustom, calls=%fused_computation.21.clone | custom fusion | bytes 66048 | tf_op jit(solution)/shard_map/jit(_take)/gather | solution.py:156
  123.1 1.2 copy.104
  126.6 1.8 gather_fusion.26
  128.6 1.2 fusion.34
  131.7 1.8 gather_fusion.27
  135.7 1.0 copy.117
  136.7 1.8 gather_fusion.28
  139.4 1.4 fusion.32
  141.8 1.6 gather_fusion.29
  143.3 1.2 copy.120
  151.1 10.0 %collective-permute-start.5 = (f32[1,8,8,128]{3,2,1,0:T(8,128)S(1)}, f32[1,8,8,128]{3,2,1,0:T(8,128)S(1)}, u32[]{:S(2)}, u32[]{:S(2)}) collective-permute-start(f32[1,8,8,128]{3,2,1,0:T(8,128)S(1)} %get-tuple-element.79), channel_id=1, source_target_pairs={{1,0},{2,1},{3,2},{4,3},{5,4},{6,5},{7,6},{8,7},{9,8},{10,9},{11,1... | collective-permute-start | bytes 98312 | tf_op jit(solution)/shard_map/ppermute | solution.py:29
  161.2 1.9 collective-permute-start.4
  164.8 3.0 %collective-permute-done.4 = f32[1,8,8,128]{3,2,1,0:T(8,128)S(1)} collective-permute-done((f32[1,8,8,128]{3,2,1,0:T(8,128)S(1)}, f32[1,8,8,128]{3,2,1,0:T(8,128)S(1)}, u32[]{:S(2)}, u32[]{:S(2)}) %collective-permute-start.4) | collective-permute-done | bytes 32800 | tf_op jit(solution)/shard_map/ppermute | solution.py:26
  177.7 11.3 %all-reduce.9 = (f32[]{:T(128)}, f32[]{:T(128)}) all-reduce(f32[]{:T(128)} %get-tuple-element.10, f32[]{:T(128)} %get-tuple-element.9), channel_id=1, replica_groups=mesh['slab_0'=8,'slab_1'=12,'slab_2'=4,'slab_3'=2] {'slab_0'}, use_global_device_ids=true, to_apply=%region_2.6 | all-reduce | flops 2 | bytes 16 | tf_op jit(solution)/shard_map/psum | solution.py:35
  189.1 16.0 %all-reduce.8 = (f32[]{:T(128)}, f32[]{:T(128)}) all-reduce(f32[]{:T(128)} %get-tuple-element.13, f32[]{:T(128)} %get-tuple-element.14), channel_id=1, replica_groups=mesh['slab_0'=8,'slab_1'=12,'slab_2'=4,'slab_3'=2] {'slab_1'}, use_global_device_ids=true, to_apply=%region_3.7 | all-reduce | flops 2 | bytes 16 | tf_op jit(solution)/shard_map/psum | solution.py:35
  205.1 15.4 %all-reduce.10 = (f32[]{:T(128)}, f32[]{:T(128)}) all-reduce(f32[]{:T(128)} %get-tuple-element.11, f32[]{:T(128)} %get-tuple-element.12), channel_id=1, replica_groups=mesh['slab_0'=8,'slab_1'=12,'slab_2'=4,'slab_3'=2] {'slab_2'}, use_global_device_ids=true, to_apply=%region_4.8 | all-reduce | flops 2 | bytes 16 | tf_op jit(solution)/shard_map/psum | solution.py:35
  220.4 12.5 %all-reduce.11 = (f32[]{:T(128)}, f32[]{:T(128)}) all-reduce(f32[]{:T(128)} %get-tuple-element.15, f32[]{:T(128)} %get-tuple-element.16), channel_id=1, replica_groups=mesh['slab_0'=8,'slab_1'=12,'slab_2'=4,'slab_3'=2] {'slab_3'}, use_global_device_ids=true, to_apply=%region_5.9 | all-reduce | flops 2 | bytes 16 | tf_op jit(solution)/shard_map/psum | solution.py:35
  (255 shorter events, 55.8 us)
Async XLA Ops:
  0.6 4.7 %copy-start.1 = (f32[3,8,8,8,128]{4,3,2,1,0:T(8,128)S(1)}, f32[3,8,8,8,128]{4,3,2,1,0:T(8,128)}, u32[]{:S(2)}) copy-start(f32[3,8,8,8,128]{4,3,2,1,0:T(8,128)} %param.12) | copy-start | bytes 2359300
  4.2 12.4 %copy-start.31 = (pred[128]{0:T(512)(128)(4,1)}, pred[128]{0:T(512)(128)(4,1)S(1)}, u32[]{:S(2)}) copy-start(pred[128]{0:T(512)(128)(4,1)S(1)} %compare_and_fusion.6) | copy-start | bytes 388
  4.2 1.1 copy-start.11
  5.7 1.0 copy-start
  9.8 1.0 copy-start.2
  17.2 27.8 %collective-permute-start.1 = (f32[2,1,8,8,128]{4,3,2,1,0:T(8,128)S(1)}, f32[2,1,8,8,128]{4,3,2,1,0:T(8,128)S(1)}, u32[]{:S(2)}, u32[]{:S(2)}) collective-permute-start(f32[2,1,8,8,128]{4,3,2,1,0:T(8,128)S(1)} %get-tuple-element.71), channel_id=1, source_target_pairs={{1,0},{2,1},{3,2},{4,3},{5,4},{6,5},{7,6},{8,7},{9,8},{10,9},{11,1... | collective-permute-start | bytes 196616 | tf_op jit(solution)/shard_map/ppermute | solution.py:29
  29.6 18.6 %collective-permute-start = (f32[2,1,8,8,128]{4,3,2,1,0:T(8,128)}, f32[2,1,8,8,128]{4,3,2,1,0:T(8,128)}, u32[]{:S(2)}, u32[]{:S(2)}) collective-permute-start(f32[2,1,8,8,128]{4,3,2,1,0:T(8,128)} %get-tuple-element.70), channel_id=1, source_target_pairs={{0,1},{1,2},{2,3},{3,4},{4,5},{5,6},{6,7},{7,8},{8,9},{9,10},{10,1... | collective-permute-start | bytes 196616 | tf_op jit(solution)/shard_map/ppermute | solution.py:26
  31.6 0.7 copy-start.39
  34.0 0.7 copy-start.37
  34.0 0.7 copy-start.38
  36.0 0.7 copy-start.34
  36.6 0.6 copy-start.36
  41.5 2.0 slice-start
  43.5 15.8 %copy-start.22 = (pred[128]{0:T(512)(128)(4,1)}, pred[128]{0:T(512)(128)(4,1)S(1)}, u32[]{:S(2)}) copy-start(pred[128]{0:T(512)(128)(4,1)S(1)} %get-tuple-element.93) | copy-start | bytes 388
  43.5 15.8 %copy-start.25 = (pred[128]{0:T(512)(128)(4,1)}, pred[128]{0:T(512)(128)(4,1)S(1)}, u32[]{:S(2)}) copy-start(pred[128]{0:T(512)(128)(4,1)S(1)} %get-tuple-element.48) | copy-start | bytes 388
  43.5 9.7 %copy-start.15 = (s32[1024]{0:T(1024)}, s32[1024]{0:T(1024)S(1)}, u32[]{:S(2)}) copy-start(s32[1024]{0:T(1024)S(1)} %pad_clamp_fusion.8) | copy-start | bytes 12292
  43.6 12.9 %copy-start.14 = (s32[1024]{0:T(1024)}, s32[1024]{0:T(1024)S(1)}, u32[]{:S(2)}) copy-start(s32[1024]{0:T(1024)S(1)} %pad_clamp_fusion.10) | copy-start | bytes 12292
  43.7 16.0 %copy-start.13 = (s32[1024]{0:T(1024)}, s32[1024]{0:T(1024)S(1)}, u32[]{:S(2)}) copy-start(s32[1024]{0:T(1024)S(1)} %pad_clamp_fusion.6) | copy-start | bytes 12292
  44.3 37.2 %copy-start.12 = (s32[1024]{0:T(1024)}, s32[1024]{0:T(1024)S(1)}, u32[]{:S(2)}) copy-start(s32[1024]{0:T(1024)S(1)} %pad_clamp_fusion.2) | copy-start | bytes 12292
  51.6 1.2 copy-start.10
  58.0 1.3 copy-start.3
  62.1 0.6 copy-start.18
  65.5 0.7 copy-start.20
  69.9 1.2 copy-start.16
  84.0 1.2 copy-start.28
  85.5 0.7 copy-start.5
  96.9 1.2 copy-start.32
  98.8 12.5 %collective-permute-start.3 = (f32[1,8,8,128]{3,2,1,0:T(8,128)S(1)}, f32[1,8,8,128]{3,2,1,0:T(8,128)S(1)}, u32[]{:S(2)}, u32[]{:S(2)}) collective-permute-start(f32[1,8,8,128]{3,2,1,0:T(8,128)S(1)} %get-tuple-element.81), channel_id=1, source_target_pairs={{1,0},{2,1},{3,2},{4,3},{5,4},{6,5},{7,6},{8,7},{9,8},{10,9},{11,1... | collective-permute-start | bytes 98312 | tf_op jit(solution)/shard_map/ppermute | solution.py:29
  109.0 10.0 %collective-permute-start.2 = (f32[1,8,8,128]{3,2,1,0:T(8,128)}, f32[1,8,8,128]{3,2,1,0:T(8,128)S(1)}, u32[]{:S(2)}, u32[]{:S(2)}) collective-permute-start(f32[1,8,8,128]{3,2,1,0:T(8,128)} %get-tuple-element.80), channel_id=1, source_target_pairs={{0,1},{1,2},{2,3},{3,4},{4,5},{5,6},{6,7},{7,8},{8,9},{9,10},{10,1... | collective-permute-start | bytes 98312 | tf_op jit(solution)/shard_map/ppermute | solution.py:26
  123.1 1.2 copy-start.23
  123.1 1.2 copy-start.26
  125.1 0.6 copy-start.6
  135.1 0.6 copy-start.7
  143.3 1.3 copy-start.8
  143.3 1.3 copy-start.29
  143.3 1.3 copy-start.4
  144.6 0.8 copy-start.9
  150.5 0.6 copy-start.33
  151.1 10.0 %copy-start.35 = (f32[8]{0:T(128)S(1)}, f32[8]{0:T(128)}, u32[]{:S(2)}) copy-start(f32[8]{0:T(128)} %or_select_fusion.1) | copy-start | bytes 100
  151.1 12.1 %collective-permute-start.5 = (f32[1,8,8,128]{3,2,1,0:T(8,128)S(1)}, f32[1,8,8,128]{3,2,1,0:T(8,128)S(1)}, u32[]{:S(2)}, u32[]{:S(2)}) collective-permute-start(f32[1,8,8,128]{3,2,1,0:T(8,128)S(1)} %get-tuple-element.79), channel_id=1, source_target_pairs={{1,0},{2,1},{3,2},{4,3},{5,4},{6,5},{7,6},{8,7},{9,8},{10,9},{11,1... | collective-permute-start | bytes 98312 | tf_op jit(solution)/shard_map/ppermute | solution.py:29
  161.2 6.6 %collective-permute-start.4 = (f32[1,8,8,128]{3,2,1,0:T(8,128)S(1)}, f32[1,8,8,128]{3,2,1,0:T(8,128)S(1)}, u32[]{:S(2)}, u32[]{:S(2)}) collective-permute-start(f32[1,8,8,128]{3,2,1,0:T(8,128)S(1)} %get-tuple-element.78), channel_id=1, source_target_pairs={{0,1},{1,2},{2,3},{3,4},{4,5},{5,6},{6,7},{7,8},{8,9},{9,10},{10,1... | collective-permute-start | bytes 98312 | tf_op jit(solution)/shard_map/ppermute | solution.py:26
  169.1 0.6 copy-start.24
  169.1 0.6 copy-start.27
  171.0 0.6 copy-start.19
  172.9 0.6 copy-start.21
  174.7 0.6 copy-start.17
  176.3 0.7 copy-start.30
where the time goes:
time: 238 us; the launch traced here: 236 us
  local copies, waits for them, and re-layouts  113 us (47%)
  blocking collectives  55.2 us (23%)
  starting transfers between devices  38.5 us (16%)
  other arithmetic  13.6 us (6%)
  matrix products  6.62 us (3%)
  waiting for transfers between devices  5.32 us (2%)
  between operations  3.3 us (1%)
    psum x4, blocking collectives, over_axes(): return functools.reduce(lax.psum, axes, shard)  55.2 us
    ppermute x3, starting transfers between devices, padded_2(): lax.ppermute(lax.slice_in_dim(block, 0, width, axis=dim), axis, backward)  32.5 us
    unnamed x91, local copies, waits for them, and re-layouts  14 us
    gather x8, local copies, waits for them, and re-layouts, assemble(): new_high = high_face + jnp.take(low_face, tables['plus_z'], axis=2)  11.1 us
    gather x8, local copies, waits for them, and re-layouts, assemble(): new_low = low_face + jnp.take(high_face, tables['minus_z'], axis=2)  11 us
    gather x8, local copies, waits for them, and re-layouts, assemble(): new_low = low_face + jnp.take(high_ext, tables['minus_x'], axis=2)  10.6 us
    gather x8, local copies, waits for them, and re-layouts, assemble(): new_high = high_face + jnp.take(low_ext, tables['plus_x'], axis=2)  10.6 us
    gather x8, local copies, waits for them, and re-layouts, boundary_faces(): high_face = jnp.take(values[-1], tables['last_cols'], axis=2)  7.42 us
  transfers between devices with their start and end apart: 6, of which 2 were waited for; matrix products, arithmetic and copies ran while one was open for 9% of the time, Pallas kernels for 0%

commit v1 on v0

v1 whole, which is shorter than its diff:
```python
import functools

import jax
import jax.numpy as jnp
import numpy as np
from jax import lax
from jax.experimental import pallas as pl
from jax.experimental.pallas import tpu as pltpu
from jax.sharding import Mesh
from jax.sharding import PartitionSpec as P

TORUS = (8, 12, 4, 2)
AXES = ("ty", "tz", "tx", "core")
NODES = 8
EL_Y = 8
EL_Z = 16
CELLS = EL_Y * EL_Z
CENTRE = 1.65
HALF = 1.35
F32 = jnp.float32


def legendre_table(positions, points):
    columns = [positions * 0.0 + 1.0, positions]
    for degree_now in range(2, points):
        columns.append(
            ((2 * degree_now - 1) * positions * columns[-1] - (degree_now - 1) * columns[-2])
            / degree_now
        )
    return np.stack(columns, axis=1)


def gll_derivative(points):
    degree = points - 1
    grid_nodes = -np.cos(np.pi * np.arange(points) / degree)
    for repeat in range(100):
        legendre = legendre_table(grid_nodes, points)
        grid_nodes = grid_nodes - (grid_nodes * legendre[:, degree] - legendre[:, degree - 1]) / (
            points * legendre[:, degree]
        )
    legendre = legendre_table(grid_nodes, points)
    top_values = legendre[:, degree]
    index_list = np.arange(points)
    same_index = index_list[:, None] == index_list[None, :]
    spacing = grid_nodes[:, None] - grid_nodes[None, :]
    spacing = np.where(same_index, 1.0, spacing)
    deriv_table = top_values[:, None] / (top_values[None, :] * spacing)
    deriv_table = np.where(same_index, 0.0, deriv_table)
    deriv_table[0, 0] = -degree * points / 4.0
    deriv_table[degree, degree] = degree * points / 4.0
    return deriv_table


DERIV = gll_derivative(NODES)
HALF_N = NODES // 2
MIRROR = DERIV[:, ::-1]
ON_SUM = 0.5 * (DERIV + MIRROR)[:HALF_N, :HALF_N]
ON_DIFF = 0.5 * (DERIV - MIRROR)[:HALF_N, :HALF_N]
SQUARED = DERIV * DERIV
SQ_SUM = 0.5 * (SQUARED + SQUARED[::-1])[:HALF_N, :HALF_N]
SQ_DIFF = 0.5 * (SQUARED - SQUARED[::-1])[:HALF_N, :HALF_N]

SIGMA = CENTRE / HALF
RHO_0 = 1.0 / SIGMA
RHO_1 = 1.0 / (2.0 * SIGMA - RHO_0)
KEEP = 1.0 + RHO_1 * RHO_0 + 2.0 * RHO_1 / HALF * CENTRE
PULL = -2.0 * RHO_1 / HALF


def combine(weights, values):
    total = None
    for weight, value in zip(weights, values):
        if weight == 0.0:
            continue
        term = value if weight == 1.0 else value * F32(weight)
        total = term if total is None else total + term
    return total


def fold(values):
    low, high = values[:HALF_N], values[: HALF_N - 1 : -1]
    return [a + b for a, b in zip(low, high)], [a - b for a, b in zip(low, high)]


def derive(values):
    even, odd = fold(values)
    by_even = [combine(ON_SUM[m], even) for m in range(HALF_N)]
    by_odd = [combine(ON_DIFF[m], odd) for m in range(HALF_N)]
    return [a + b for a, b in zip(by_even, by_odd)] + [
        b - a for a, b in zip(by_even[::-1], by_odd[::-1])
    ]


def derive_back(values):
    even, odd = fold(values)
    by_even = [combine(ON_DIFF[:, a], even) for a in range(HALF_N)]
    by_odd = [combine(ON_SUM[:, a], odd) for a in range(HALF_N)]
    return [a + b for a, b in zip(by_even, by_odd)] + [
        b - a for a, b in zip(by_even[::-1], by_odd[::-1])
    ]


def square_back(values):
    even, odd = fold(values)
    by_even = [combine(SQ_SUM[:, a], even) for a in range(HALF_N)]
    by_odd = [combine(SQ_DIFF[:, a], odd) for a in range(HALF_N)]
    return [a + b for a, b in zip(by_even, by_odd)] + [
        a - b for a, b in zip(by_even[::-1], by_odd[::-1])
    ]


def stiff_line(values, factors):
    return derive_back([g * d for g, d in zip(factors, derive(values))])


def lanes_of(value, index):
    return jnp.take_along_axis(value, index, axis=1, mode="promise_in_bounds")


class Shared:
    def __init__(self):
        lane = lax.broadcasted_iota(jnp.int32, (8, 128), 1)
        row = lax.broadcasted_iota(jnp.int32, (8, 128), 0)
        pos_z = lane % EL_Z
        up = lane - pos_z + (pos_z + 1) % EL_Z
        down = lane - pos_z + (pos_z + EL_Z - 1) % EL_Z
        self.across = jnp.where(row == 0, up, down)
        self.has_low = lane >= EL_Z
        self.has_high = lane < CELLS - EL_Z
        self.first = row == 0
        self.last = row == NODES - 1

    def plane(self, rows):
        low, high = rows[0], rows[-1]
        zero = jnp.zeros_like(low)
        new_low = low + jnp.where(self.has_low, pltpu.roll(high, EL_Z, 1), zero)
        new_high = high + jnp.where(self.has_high, pltpu.roll(low, CELLS - EL_Z, 1), zero)
        out = []
        for value in [new_low, *rows[1:-1], new_high]:
            moved = lanes_of(value, self.across)
            from_last = pltpu.roll(moved, 1, 0)
            from_first = pltpu.roll(moved, NODES - 1, 0)
            added = jnp.where(self.first, from_last, jnp.where(self.last, from_first, zero))
            out.append(value + added)
        return out


def rows_of(ref, *at):
    return [ref[(*at, pl.ds(8 * b, 8), slice(None))] for b in range(NODES)]


def put_rows(ref, values, *at):
    for b, value in enumerate(values):
        ref[(*at, pl.ds(8 * b, 8), slice(None))] = value


def turned(ref, *at):
    return [ref[(*at, pl.ds(c, 8, stride=8), slice(None))] for c in range(NODES)]


def prepare(core_ref, order_ref, load_in, geom_in, mass_in, load, geo_a, geo_b, geo_c, mass, diag, lead, message, raw, sems):
    sources = [geom_in.at[0], geom_in.at[1], geom_in.at[2], mass_in, load_in]
    copies = [pltpu.make_async_copy(src, raw.at[i], sems.at[i]) for i, src in enumerate(sources)]
    for copy in copies:
        copy.start()
    core = core_ref[0]
    cells = jnp.broadcast_to(order_ref[...], (CELLS, CELLS))
    hot = (cells == lax.broadcasted_iota(jnp.int32, (CELLS, CELLS), 0)).astype(F32)
    column = lax.broadcasted_iota(jnp.int32, (8, CELLS), 1).astype(F32)
    index = lax.dot_general(column, hot, (((1,), (1,)), ((), ())), preferred_element_type=F32)
    index = index.astype(jnp.int32)
    at = [a + core * (NODES - 1 - 2 * a) for a in range(NODES)]

    def fetch(which, a):
        return [lanes_of(v, index) for v in rows_of(raw, which, at[a])]

    copies[0].wait()
    for a in range(NODES):
        put_rows(geo_a, fetch(0, a), a)
    copies[1].wait()
    for a in range(NODES):
        put_rows(geo_b, fetch(1, a), a)
    copies[2].wait()
    for a in range(NODES):
        for c in range(NODES):
            geo_c[a, pl.ds(8 * c, 8), :] = lanes_of(raw[2, at[a], pl.ds(c, 8, stride=8), :], index)
    copies[3].wait()
    for a in range(NODES):
        put_rows(mass, fetch(3, a), a)
    copies[4].wait()
    for a in range(NODES):
        put_rows(load, fetch(4, a), a)
    for a in range(1, NODES):
        put_rows(diag, square_back(rows_of(geo_c, a)), a)
    for a in range(1, NODES):
        part = square_back(rows_of(geo_b, a))
        turn = turned(diag, a)
        put_rows(diag, [x + y + z for x, y, z in zip(part, turn, rows_of(mass, a))], a)
    for b in range(NODES):
        here = pl.ds(8 * b, 8)
        part = square_back([geo_a[a, here, :] for a in range(NODES)])
        lead[here, :] = part[0] + mass[0, here, :]
        for a in range(1, NODES):
            diag[a, here, :] = diag[a, here, :] + part[a]
    put_rows(message, rows_of(load, NODES - 1), 0)
    put_rows(message, rows_of(diag, NODES - 1), 1)


def begin(load, geo_a, geo_b, geo_c, diag, lead, pair, start, recip, first, slope, message):
    shared = Shared()
    for a in range(1, NODES):
        if a < NODES - 1:
            top, low = rows_of(load, a), rows_of(diag, a)
        else:
            top = [x + y for x, y in zip(rows_of(pair, 0, 0), rows_of(pair, 1, 0))]
            low = [x + y for x, y in zip(rows_of(pair, 0, 1), rows_of(pair, 1, 1))]
        top, low = shared.plane(top), [1.0 / v for v in shared.plane(low)]
        put_rows(start, top, a)
        put_rows(recip, low, a)
        put_rows(first, [x * y * F32(1.0 / CENTRE) for x, y in zip(top, low)], a)
    for b in range(NODES):
        here = pl.ds(8 * b, 8)
        zero = jnp.zeros((8, 128), F32)
        grad = derive([zero] + [first[a, here, :] for a in range(1, NODES)])
        for a in range(NODES):
            slope[a, here, :] = grad[a]
        flux = [geo_a[a, here, :] * grad[a] for a in range(NODES)]
        message[1, here, :] = combine(DERIV[:, 0], flux)
    put_rows(message, rows_of(load, 0), 0)
    put_rows(message, [lead[pl.ds(8 * b, 8), :] for b in range(NODES)], 2)
    put_rows(message, rows_of(geo_b, 0), 3)
    put_rows(message, rows_of(geo_c, 0), 4)


def middle(both, geo_a, geo_b, geo_c, mass, recip_in, first_in, slope, start0, recip0, first0, local, precond, message, work):
    shared = Shared()

    def summed(which):
        return [x + y for x, y in zip(rows_of(both, 0, which), rows_of(both, 1, which))]

    lead, fac_b, fac_c = summed(2), summed(3), summed(4)
    put_rows(work, square_back(fac_c), 0)
    low = [x + y + z for x, y, z in zip(square_back(fac_b), turned(work, 0), lead)]
    low = [1.0 / v for v in shared.plane(low)]
    top = shared.plane(summed(0))
    head = [x * y * F32(1.0 / CENTRE) for x, y in zip(top, low)]
    put_rows(start0, top)
    put_rows(recip0, low)
    put_rows(first0, head)
    put_rows(work, stiff_line(turned(first0), fac_c), 0)
    turn = turned(work, 0)
    part = stiff_line(head, fac_b)
    image = [r + k * u + x + y for r, k, u, x, y in zip(summed(1), lead, head, part, turn)]
    image = shared.plane(image)
    put_rows(precond, [u * F32(KEEP) + q * d * F32(PULL) for u, q, d in zip(head, image, low)], 0)

    for b in range(NODES):
        here = pl.ds(8 * b, 8)
        flux = []
        for a in range(NODES):
            flux.append(geo_a[a, here, :] * (slope[a, here, :] + head[b] * F32(DERIV[a, 0])))
        back = derive_back(flux)
        for a in range(1, NODES):
            local[a, here, :] = back[a]
    for a in range(1, NODES):
        put_rows(work, stiff_line(turned(first_in, a), rows_of(geo_c, a)), a)
    for a in range(1, NODES):
        values = rows_of(first_in, a)
        part = stiff_line(values, rows_of(geo_b, a))
        turn = turned(work, a)
        image = [
            x + y + z + m * v
            for x, y, z, m, v in zip(rows_of(local, a), part, turn, rows_of(mass, a), values)
        ]
        if a == NODES - 1:
            put_rows(message, image)
        else:
            image = shared.plane(image)
            low = rows_of(recip_in, a)
            put_rows(
                precond,
                [u * F32(KEEP) + q * d * F32(PULL) for u, q, d in zip(values, image, low)],
                a,
            )


def finish(pair, geo_a, geo_b, geo_c, mass, load, recip_in, first_in, precond_in, last, image, outer, inner, row, local, work):
    shared = Shared()
    whole = shared.plane([x + y for x, y in zip(rows_of(pair, 0), rows_of(pair, 1))])
    end = [
        u * F32(KEEP) + q * d * F32(PULL)
        for u, q, d in zip(rows_of(first_in, NODES - 1), whole, rows_of(recip_in, NODES - 1))
    ]
    put_rows(last, end)

    def iterate(a):
        return rows_of(last) if a == NODES - 1 else rows_of(precond_in, a)

    for b in range(NODES):
        here = pl.ds(8 * b, 8)
        values = [precond_in[a, here, :] for a in range(NODES - 1)] + [end[b]]
        back = stiff_line(values, [geo_a[a, here, :] for a in range(NODES)])
        for a in range(NODES):
            local[a, here, :] = back[a]
    for a in range(NODES):
        lines = turned(last) if a == NODES - 1 else turned(precond_in, a)
        put_rows(work, stiff_line(lines, rows_of(geo_c, a)), a)
    over = [jnp.zeros((8, 128), F32) for _ in range(NODES)]
    under = [jnp.zeros((8, 128), F32) for _ in range(NODES)]
    for a in range(NODES):
        values = iterate(a)
        part = stiff_line(values, rows_of(geo_b, a))
        turn = turned(work, a)
        total = [
            x + y + z + m * v
            for x, y, z, m, v in zip(rows_of(local, a), part, turn, rows_of(mass, a), values)
        ]
        over = [s + v * f for s, v, f in zip(over, values, rows_of(load, a))]
        under = [s + v * t for s, v, t in zip(under, values, total)]
        if a == 0:
            put_rows(outer, total)
        elif a == NODES - 1:
            put_rows(inner, total)
        else:
            put_rows(image, shared.plane(total), a)
    over = jnp.sum(functools.reduce(jnp.add, over), axis=0, keepdims=True)
    under = jnp.sum(functools.reduce(jnp.add, under), axis=0, keepdims=True)
    over = over + pltpu.roll(over, 64, 1)
    under = under + pltpu.roll(under, 64, 1)
    lane = lax.broadcasted_iota(jnp.int32, (1, 128), 1)
    row[...] = jnp.broadcast_to(jnp.where(lane < 64, over, under), row.shape)


def close(core_ref, order_ref, sums, outer, outer_other, pair, start_in, start0, precond_in, last, image_in, solution_out, residual_out, buf_s, buf_r, sems):
    shared = Shared()
    core = core_ref[0]
    index = jnp.broadcast_to(order_ref[...], (8, CELLS))
    lane = lax.broadcasted_iota(jnp.int32, (1, 128), 1)
    total = jnp.sum(sums[...], axis=0, keepdims=True)
    zero = jnp.zeros_like(total)
    over = jnp.sum(jnp.where(lane < 64, total, zero), axis=1, keepdims=True)
    under = jnp.sum(jnp.where(lane < 64, zero, total), axis=1, keepdims=True)
    alpha = jnp.broadcast_to(over / under, (8, 128))
    at = [a + core * (NODES - 1 - 2 * a) for a in range(NODES)]
    copies = []
    for a in range(NODES):
        if a == 0:
            head, values = rows_of(start0), rows_of(precond_in, 0)
            image = shared.plane([x + y for x, y in zip(rows_of(outer), rows_of(outer_other))])
        elif a == NODES - 1:
            head, values = rows_of(start_in, a), rows_of(last)
            image = shared.plane([x + y for x, y in zip(rows_of(pair, 0), rows_of(pair, 1))])
        else:
            head, values, image = rows_of(start_in, a), rows_of(precond_in, a), rows_of(image_in, a)
        put_rows(buf_s, [lanes_of(alpha * v, index) for v in values], a)
        put_rows(buf_r, [lanes_of(s - alpha * i, index) for s, i in zip(head, image)], a)
        for i, (buf, out) in enumerate(((buf_s, solution_out), (buf_r, residual_out))):
            copy = pltpu.make_async_copy(buf.at[a], out.at[at[a]], sems.at[i, a])
            copy.start()
            copies.append(copy)
    for copy in copies:
        copy.wait()


VMEM = pl.BlockSpec(memory_space=pltpu.VMEM)
SMEM = pl.BlockSpec(memory_space=pltpu.SMEM)
ANY = pl.BlockSpec(memory_space=pl.ANY)
FIELD = (NODES, 64, 128)
FACE = (64, 128)


def call(body, name, outs, ins, scratch=(), out_specs=None, flops=4_000_000):
    return pl.pallas_call(
        body,
        name=name,
        out_shape=[jax.ShapeDtypeStruct(s, F32) for s in outs],
        in_specs=ins,
        out_specs=out_specs or [VMEM] * len(outs),
        scratch_shapes=list(scratch),
        compiler_params=pltpu.CompilerParams(vmem_limit_bytes=12 << 20),
        cost_estimate=pl.CostEstimate(flops=flops, bytes_accessed=2 << 20, transcendentals=0),
    )


def on_device(load_terms, geometry, mass_terms, element_order):
    count = 1
    for axis in AXES:
        count *= lax.axis_size(axis)
    across_chips = [[2 * k + 1, (2 * k + 2) % count] for k in range(count // 2)]
    swap = [(i, (i + 1) % count if i % 2 else (i - 1) % count) for i in range(count)]
    core = lax.axis_index("core").astype(jnp.int32).reshape(1)
    field = jax.ShapeDtypeStruct(FIELD, F32)
    dma = pltpu.SemaphoreType.DMA
    load_terms = load_terms.reshape(FIELD)
    geometry = geometry.reshape(3, *FIELD)
    mass_terms = mass_terms.reshape(FIELD)

    load, geo_a, geo_b, geo_c, mass, diag, lead, message = call(
        prepare,
        "prepare",
        [FIELD] * 6 + [FACE, (2, *FACE)],
        [SMEM, VMEM, ANY, ANY, ANY],
        [pltpu.VMEM((5, *FIELD), F32), dma((5,))],
    )(core, element_order, load_terms, geometry, mass_terms)
    pair = lax.all_gather(message, "core")
    start, recip, first, slope, message = call(
        begin, "begin", [FIELD] * 4 + [(5, *FACE)], [VMEM] * 7
    )(load, geo_a, geo_b, geo_c, diag, lead, pair)
    both = lax.all_gather(message, AXES, axis_index_groups=across_chips)
    start0, recip0, first0, local, precond, message = call(
        middle,
        "middle",
        [FACE] * 3 + [FIELD, FIELD, FACE],
        [VMEM] * 8,
        [pltpu.VMEM(FIELD, F32)],
    )(both, geo_a, geo_b, geo_c, mass, recip, first, slope)
    pair = lax.all_gather(message, "core")
    group = lax.axis_size("ty") * lax.axis_size("tx")
    last, image, outer, inner, row = call(
        finish,
        "finish",
        [FACE, FIELD, FACE, FACE, (group, 128)],
        [VMEM] * 9,
        [pltpu.VMEM(FIELD, F32), pltpu.VMEM(FIELD, F32)],
    )(pair, geo_a, geo_b, geo_c, mass, load, recip, first, precond)
    outer_other = lax.ppermute(outer, AXES, swap)
    pair = lax.all_gather(inner, "core")
    sums = lax.all_to_all(row, ("ty", "tx"), 0, 0, tiled=True)
    group = lax.axis_size("tz") * lax.axis_size("core")
    row = jnp.broadcast_to(jnp.sum(sums, axis=0, keepdims=True), (group, 128))
    sums = lax.all_to_all(row, ("tz", "core"), 0, 0, tiled=True)
    solution, residual = call(
        close,
        "close",
        [FIELD, FIELD],
        [SMEM] + [VMEM] * 10,
        [pltpu.VMEM(FIELD, F32), pltpu.VMEM(FIELD, F32), dma((2, NODES))],
        out_specs=[ANY, ANY],
    )(core, element_order, sums, outer, outer_other, pair, start, start0, precond, last, image)
    shape = (NODES, NODES, NODES, CELLS)
    return solution.reshape(shape), residual.reshape(shape)


def solution(mesh):
    torus = Mesh(mesh.devices.reshape(TORUS), AXES)
    placed = (
        P(None, None, None, AXES),
        P(None, None, None, None, AXES),
        P(None, None, None, AXES),
        P(AXES, None),
    )
    return jax.shard_map(
        on_device,
        mesh=torus,
        in_specs=placed,
        out_specs=(P(None, None, None, AXES), P(None, None, None, AXES)),
        check_vma=False,
    )
```

time: 238 us -> 68.1 us (0.29)
  local copies, waits for them, and re-layouts: 113 us -> 4.29 us
  starting transfers between devices: 38.5 us -> 11.7 us
  other arithmetic: 13.6 us -> 0.05 us
  blocking collectives: 55.2 us -> 43.6 us
  matrix products: 6.62 us -> 0 us
  Pallas kernels: 0 us -> 5.11 us
  waiting for transfers between devices: 5.32 us -> 2.3 us
  between operations: 3.3 us -> 0.68 us
    gather x70 -> x0, local copies, waits for them, and re-layouts: 76.7 us -> none  [the longest x8 11.1 us: assemble(): new_high = high_face + jnp.take(low_face, tables['plus_z'], axis=2)]
    psum x4 -> x0, blocking collectives: 55.2 us -> none  [over_axes(): return functools.reduce(lax.psum, axes, shard)]
    ppermute x6 -> x1, starting transfers between devices: 38.5 us -> 2.28 us  [on_device(): outer_other = lax.ppermute(outer, AXES, swap)]
    all_gather x0 -> x4, blocking collectives: none -> 30.9 us  [the longest x2 20.7 us: on_device(): pair = lax.all_gather(message, 'core')]
    squeeze x22 -> x0, local copies, waits for them, and re-layouts: 13.1 us -> none  [the longest x5 3.33 us: assemble(): high_face = values[:, :, -1]]
    all_to_all x0 -> x1, blocking collectives: none -> 12.7 us  [on_device(): sums = lax.all_to_all(row, ('ty', 'tx'), 0, 0, tiled=True)]
    unnamed x91 -> x8, local copies, waits for them, and re-layouts: 14 us -> 3.68 us
    all_to_all x0 -> x1, starting transfers between devices: none -> 9.42 us  [on_device(): sums = lax.all_to_all(row, ('tz', 'core'), 0, 0, tiled=True)]
  transfers between devices with their start and end apart: 6 -> 2, of which waited for: 2 -> 1; matrix products, arithmetic and copies ran while one was open for 9% -> 0% of each run, Pallas kernels for 0% -> 0%
where the time goes in v1:
time: 68.1 us; the launch traced here: 67.7 us
  blocking collectives  43.6 us (64%)
  starting transfers between devices  11.7 us (17%)
  Pallas kernels  5.11 us (8%)
  local copies, waits for them, and re-layouts  4.29 us (6%)
  waiting for transfers between devices  2.3 us (3%)
    all_gather x2, blocking collectives, on_device(): pair = lax.all_gather(message, 'core')  20.7 us
    all_to_all x1, blocking collectives, on_device(): sums = lax.all_to_all(row, ('ty', 'tx'), 0, 0, tiled=True)  12.7 us
    all_to_all x1, starting transfers between devices, on_device(): sums = lax.all_to_all(row, ('tz', 'core'), 0, 0, tiled=True)  9.42 us
    all_gather x1, blocking collectives, on_device(): both = lax.all_gather(message, AXES, axis_index_groups=across_chips)  5.43 us
    all_gather x1, blocking collectives, on_device(): pair = lax.all_gather(inner, 'core')  4.78 us
    unnamed x8, local copies, waits for them, and re-layouts  3.68 us
    all_to_all x1, waiting for transfers between devices, on_device(): sums = lax.all_to_all(row, ('tz', 'core'), 0, 0, tiled=True)  2.3 us
    ppermute x1, starting transfers between devices, on_device(): outer_other = lax.ppermute(outer, AXES, swap)  2.28 us
  transfers between devices with their start and end apart: 2, of which 1 were waited for; matrix products, arithmetic and copies ran while one was open for 0% of the time, Pallas kernels for 0%

profile of v1, /device:TPU:1, one launch (start us, length us, event | category | flops | bytes accessed | tf_op | source)
XLA Modules:
  0.0 67.7 jit_solution(14567762323018016983)
XLA Ops:
  0.6 0.0 copy-start.3
  0.6 0.6 copy-done.3
  1.3 0.0 copy-start
  1.3 1.1 %copy-done = f32[3,8,8,8,128]{4,3,2,1,0:T(8,128)S(1)} copy-done((f32[3,8,8,8,128]{4,3,2,1,0:T(8,128)S(1)}, f32[3,8,8,8,128]{4,3,2,1,0:T(8,128)}, u32[]{:S(2)}) %copy-start) | copy-done | bytes 786456
  2.4 0.0 copy-start.1
  2.4 0.9 %copy-done.1 = f32[8,8,8,128]{3,2,1,0:T(8,128)S(1)} copy-done((f32[8,8,8,128]{3,2,1,0:T(8,128)S(1)}, f32[8,8,8,128]{3,2,1,0:T(8,128)}, u32[]{:S(2)}) %copy-start.1) | copy-done | bytes 262168
  3.4 0.0 copy-start.2
  3.4 0.9 %copy-done.2 = f32[8,8,8,128]{3,2,1,0:T(8,128)S(1)} copy-done((f32[8,8,8,128]{3,2,1,0:T(8,128)S(1)}, f32[8,8,8,128]{3,2,1,0:T(8,128)}, u32[]{:S(2)}) %copy-start.2) | copy-done | bytes 262168
  4.3 1.1 %prepare.1 = (f32[8,64,128]{2,1,0:T(8,128)S(1)}, f32[8,64,128]{2,1,0:T(8,128)S(1)}, f32[8,64,128]{2,1,0:T(8,128)S(1)}, f32[8,64,128]{2,1,0:T(8,128)S(1)}, f32[8,...) custom-call(s32[1]{0:T(128)} %bitcast.core_ref, ...), custom_call_target="tpu_custom_call" | custom-call | flops 4000000 | bytes 2097152 | tf_op jit(solution)/shard_map/prepare/pallas_call | solution.py:398
  5.4 12.0 %all-gather = f32[4,64,128]{2,1,0:T(8,128)S(1)} all-gather(f32[2,64,128]{2,1,0:T(8,128)S(1)} %get-tuple-element.31), channel_id=2, replica_groups=mesh['ty'=8,'tz'=12,'tx'=4,'core'=2] {'core'}, dimensions={0}, use_global_device_ids=true | all-gather | bytes 196608 | tf_op jit(solution)/shard_map/all_gather | solution.py:405
  17.5 0.6 begin.1
  18.0 5.4 %all-gather.1 = f32[10,64,128]{2,1,0:T(8,128)S(1)} all-gather(f32[5,64,128]{2,1,0:T(8,128)S(1)} %get-tuple-element.32), channel_id=3, replica_groups={{1,2},{3,4},{5,6},{7,8},{9,10},{11,12},{13,14},{15,16},{17,18},{19,20},..., dimensions={0}, use_global_device_ids=true | all-gather | bytes 491520 | tf_op jit(solution)/shard_map/all_gather | solution.py:409
  23.5 1.3 %middle.1 = (f32[64,128]{1,0:T(8,128)S(1)}, f32[64,128]{1,0:T(8,128)}, f32[64,128]{1,0:T(8,128)}, f32[8,64,128]{2,1,0:T(8,128)}, f32[8,64,128]{2,1,0:T(8,128)S(1)}, /*index=5*/f32[64,128]{1,0:T(8,128)S(1)}) custom-call(f32[2,5,64,128]{3,2,1,0:T(8,128)S(1)} %bitcast.14, f32[8,64,128]{2,1,0:T(8,128)S(1)} %get-tuple-element.26.geo_a, ...), custom_call_target="tpu_custom_call" | custom-call | flops 4000000 | bytes 2097152 | tf_op jit(solution)/shard_map/middle/pallas_call | solution.py:410
  24.8 8.6 %all-gather.2 = f32[128,128]{1,0:T(8,128)S(1)} all-gather(f32[64,128]{1,0:T(8,128)S(1)} %get-tuple-element.37), channel_id=4, replica_groups=mesh['ty'=8,'tz'=12,'tx'=4,'core'=2] {'core'}, dimensions={0}, use_global_device_ids=true | all-gather | bytes 98304 | tf_op jit(solution)/shard_map/all_gather | solution.py:417
  33.4 0.8 %finish.1 = (f32[64,128]{1,0:T(8,128)S(1)}, f32[8,64,128]{2,1,0:T(8,128)S(1)}, f32[64,128]{1,0:T(8,128)S(1)}, f32[64,128]{1,0:T(8,128)S(1)}, f32[32,128]{1,0:T(8,128)S(1)}) custom-call(f32[2,64,128]{2,1,0:T(8,128)S(1)} %bitcast.18, f32[8,64,128]{2,1,0:T(8,128)S(1)} %get-tuple-element.26.geo_a, f32[8,64,128]{2,1,0:T(8,128)S(1)} %get-tuple-element.27.geo_b, ...), custom_call_target="tpu_custom_call" | custom-call | flops 4000000 | bytes 2097152 | tf_op jit(solution)/shard_map/finish/pallas_call | solution.py:419
  34.2 12.7 %all_to_all.17 = f32[32,1,128]{2,1,0:T(1,128)S(1)} all-to-all(f32[32,1,128]{2,1,0:T(1,128)S(1)} %bitcast.22), channel_id=1, replica_groups=mesh['ty'=8,'tz'=12,'tx'=4,'core'=2] {'ty','tx'}, dimensions={0} | all-to-all | bytes 32768 | tf_op jit(solution)/shard_map/all_to_all | solution.py:428
  46.9 0.1 reduce_sum.9
  46.9 0.6 broadcast_in_dim.2
  47.5 9.4 %all-to-all-start.1 = ((f32[24,1,128]{2,1,0:T(1,128)}), f32[24,1,128]{2,1,0:T(1,128)S(1)}, u32[]{:S(2)}, u32[]{:S(2)}) async-start(f32[24,1,128]{2,1,0:T(1,128)} %broadcast_in_dim.2), calls=%async_computation.1 | async-start | bytes 24576 | tf_op jit(solution)/shard_map/all_to_all | solution.py:431
  57.0 2.3 %collective-permute-start = (f32[64,128]{1,0:T(8,128)S(1)}, f32[64,128]{1,0:T(8,128)S(1)}, u32[]{:S(2)}, u32[]{:S(2)}) collective-permute-start(f32[64,128]{1,0:T(8,128)S(1)} %get-tuple-element.40.outer), channel_id=1, source_target_pairs={{0,767},{1,2},{2,1},{3,4},{4,3},{5,6},{6,5},{7,8},{8,7},{9,10},{10... | collective-permute-start | bytes 98312 | tf_op jit(solution)/shard_map/ppermute | solution.py:426
  59.3 4.8 %all-gather.3 = f32[128,128]{1,0:T(8,128)S(1)} all-gather(f32[64,128]{1,0:T(8,128)S(1)} %get-tuple-element.41), channel_id=5, replica_groups=mesh['ty'=8,'tz'=12,'tx'=4,'core'=2] {'core'}, dimensions={0}, use_global_device_ids=true | all-gather | bytes 98304 | tf_op jit(solution)/shard_map/all_gather | solution.py:427
  64.0 0.0 collective-permute-done.outer_other
  64.0 2.3 %all-to-all-done.1 = f32[24,1,128]{2,1,0:T(1,128)S(1)} async-done(((f32[24,1,128]{2,1,0:T(1,128)}), f32[24,1,128]{2,1,0:T(1,128)S(1)}, u32[]{:S(2)}, u32[]{:S(2)}) %all-to-all-start.1) | async-done | bytes 12320 | tf_op jit(solution)/shard_map/all_to_all | solution.py:431
  66.3 1.4 %close.1 = (f32[8,64,128]{2,1,0:T(8,128)}, f32[8,64,128]{2,1,0:T(8,128)}) custom-call(s32[1]{0:T(128)} %bitcast.core_ref, s32[1,128]{1,0:T(1,128)S(1)} %copy-done.3, f32[24,128]{1,0:T(8,128)S(1)} %bitcast.21, f32[64,128]{1,0:T(8,128)S(1)} %get-tuple-element.40.outer, f32[64,128]{1,0:T(8,128)S(1)} %collective-permute-done.outer_other, ...), custom_call_target="tpu_custom_call" | custom-call | flops 4000000 | bytes 2097152 | tf_op jit(solution)/shard_map/close/pallas_call | solution.py:432
Async XLA Ops:
  0.6 0.7 copy-start.3
  1.3 1.1 %copy-start = (f32[3,8,8,8,128]{4,3,2,1,0:T(8,128)S(1)}, f32[3,8,8,8,128]{4,3,2,1,0:T(8,128)}, u32[]{:S(2)}) copy-start(f32[3,8,8,8,128]{4,3,2,1,0:T(8,128)} %param.5) | copy-start | bytes 2359300
  2.4 0.9 %copy-start.1 = (f32[8,8,8,128]{3,2,1,0:T(8,128)S(1)}, f32[8,8,8,128]{3,2,1,0:T(8,128)}, u32[]{:S(2)}) copy-start(f32[8,8,8,128]{3,2,1,0:T(8,128)} %param.4) | copy-start | bytes 786436
  3.4 0.9 %copy-start.2 = (f32[8,8,8,128]{3,2,1,0:T(8,128)S(1)}, f32[8,8,8,128]{3,2,1,0:T(8,128)}, u32[]{:S(2)}) copy-start(f32[8,8,8,128]{3,2,1,0:T(8,128)} %param.6) | copy-start | bytes 786436
  47.5 18.8 %all-to-all-start.1 = ((f32[24,1,128]{2,1,0:T(1,128)}), f32[24,1,128]{2,1,0:T(1,128)S(1)}, u32[]{:S(2)}, u32[]{:S(2)}) async-start(f32[24,1,128]{2,1,0:T(1,128)} %broadcast_in_dim.2), calls=%async_computation.1 | async-start | bytes 24576 | tf_op jit(solution)/shard_map/all_to_all | solution.py:431
  57.0 7.1 %collective-permute-start = (f32[64,128]{1,0:T(8,128)S(1)}, f32[64,128]{1,0:T(8,128)S(1)}, u32[]{:S(2)}, u32[]{:S(2)}) collective-permute-start(f32[64,128]{1,0:T(8,128)S(1)} %get-tuple-element.40.outer), channel_id=1, source_target_pairs={{0,767},{1,2},{2,1},{3,4},{4,3},{5,6},{6,5},{7,8},{8,7},{9,10},{10... | collective-permute-start | bytes 98312 | tf_op jit(solution)/shard_map/ppermute | solution.py:426

commit v2 on v1

--- a/solution.py
+++ b/solution.py
@@ -9,8 +9,19 @@
 from jax.sharding import Mesh
 from jax.sharding import PartitionSpec as P
 
+
 TORUS = (8, 12, 4, 2)
 AXES = ("ty", "tz", "tx", "core")
+ROOT = (6, 10, 2, 1)
+
+
+def groups(axes):
+    ids = np.arange(np.prod(TORUS)).reshape(TORUS)
+    ids = np.roll(ids, [-r for r in ROOT], range(4))
+    others = [d for d in range(4) if d not in axes]
+    return ids.transpose(*others, *axes).reshape(-1, np.prod([TORUS[d] for d in axes])).tolist()
+
+
 NODES = 8
 EL_Y = 8
 EL_Z = 16
@@ -33,7 +44,7 @@
 def gll_derivative(points):
     degree = points - 1
     grid_nodes = -np.cos(np.pi * np.arange(points) / degree)
-    for repeat in range(100):
+    for _ in range(100):
         legendre = legendre_table(grid_nodes, points)
         grid_nodes = grid_nodes - (grid_nodes * legendre[:, degree] - legendre[:, degree - 1]) / (
             points * legendre[:, degree]
@@ -158,12 +169,15 @@
     return [ref[(*at, pl.ds(c, 8, stride=8), slice(None))] for c in range(NODES)]
 
 
-def prepare(core_ref, order_ref, load_in, geom_in, mass_in, load, geo_a, geo_b, geo_c, mass, diag, lead, message, raw, sems):
+def prepare(order_in, load_in, geom_in, mass_in, load, geo_a, geo_b, geo_c, mass, diag, lead, message, order_ref, raw, sems):
+    order_copy = pltpu.make_async_copy(order_in, order_ref, sems.at[5])
+    order_copy.start()
     sources = [geom_in.at[0], geom_in.at[1], geom_in.at[2], mass_in, load_in]
     copies = [pltpu.make_async_copy(src, raw.at[i], sems.at[i]) for i, src in enumerate(sources)]
     for copy in copies:
         copy.start()
-    core = core_ref[0]
+    core = lax.axis_index("core")
+    order_copy.wait()
     cells = jnp.broadcast_to(order_ref[...], (CELLS, CELLS))
     hot = (cells == lax.broadcasted_iota(jnp.int32, (CELLS, CELLS), 0)).astype(F32)
     column = lax.broadcasted_iota(jnp.int32, (8, CELLS), 1).astype(F32)
@@ -190,9 +204,9 @@
     copies[4].wait()
     for a in range(NODES):
         put_rows(load, fetch(4, a), a)
-    for a in range(1, NODES):
+    for a in range(1, NODES - 1):
         put_rows(diag, square_back(rows_of(geo_c, a)), a)
-    for a in range(1, NODES):
+    for a in range(1, NODES - 1):
         part = square_back(rows_of(geo_b, a))
         turn = turned(diag, a)
         put_rows(diag, [x + y + z for x, y, z in zip(part, turn, rows_of(mass, a))], a)
@@ -200,21 +214,47 @@
         here = pl.ds(8 * b, 8)
         part = square_back([geo_a[a, here, :] for a in range(NODES)])
         lead[here, :] = part[0] + mass[0, here, :]
-        for a in range(1, NODES):
+        for a in range(1, NODES - 1):
             diag[a, here, :] = diag[a, here, :] + part[a]
-    put_rows(message, rows_of(load, NODES - 1), 0)
-    put_rows(message, rows_of(diag, NODES - 1), 1)
-
-
-def begin(load, geo_a, geo_b, geo_c, diag, lead, pair, start, recip, first, slope, message):
+        message[1, here, :] = part[NODES - 1]
+    for i, ref in ((0, load), (2, mass), (3, geo_b), (4, geo_c)):
+        put_rows(message, rows_of(ref, NODES - 1), i)
+
+
+def summed(ref, which):
+    return [x + y for x, y in zip(rows_of(ref, 0, which), rows_of(ref, 1, which))]
+
+
+def settle(shared, load, lead, fac_b, fac_c, work):
+    put_rows(work, square_back(fac_c))
+    low = [x + y + z for x, y, z in zip(square_back(fac_b), turned(work), lead)]
+    low = [1.0 / v for v in shared.plane(low)]
+    top = shared.plane(load)
+    return top, low, [x * y * F32(1.0 / CENTRE) for x, y in zip(top, low)]
+
+
+def within(values, lead, fac_b, fac_c, keep, work):
+    put_rows(keep, values)
+    put_rows(work, stiff_line(turned(keep), fac_c))
+    part = stiff_line(values, fac_b)
+    return [k * u + x + y for k, u, x, y in zip(lead, values, part, turned(work))]
+
+
+def begin(load, geo_a, geo_b, geo_c, diag, lead, pair, start, recip, first, slope, message, end, keep, work):
     shared = Shared()
-    for a in range(1, NODES):
-        if a < NODES - 1:
-            top, low = rows_of(load, a), rows_of(diag, a)
-        else:
-            top = [x + y for x, y in zip(rows_of(pair, 0, 0), rows_of(pair, 1, 0))]
-            low = [x + y for x, y in zip(rows_of(pair, 0, 1), rows_of(pair, 1, 1))]
-        top, low = shared.plane(top), [1.0 / v for v in shared.plane(low)]
+    mass_7, fac_b, fac_c = summed(pair, 2), summed(pair, 3), summed(pair, 4)
+    lead_7 = [x + y for x, y in zip(summed(pair, 1), mass_7)]
+    top, low, tail = settle(shared, summed(pair, 0), lead_7, fac_b, fac_c, work)
+    put_rows(start, top, NODES - 1)
+    put_rows(recip, low, NODES - 1)
+    put_rows(first, tail, NODES - 1)
+    put_rows(end, lead_7, 0)
+    put_rows(end, fac_b, 1)
+    put_rows(end, fac_c, 2)
+    put_rows(end, within(tail, mass_7, fac_b, fac_c, keep, work), 3)
+    for a in range(1, NODES - 1):
+        top, low = shared.plane(rows_of(load, a)), shared.plane(rows_of(diag, a))
+        low = [1.0 / v for v in low]
         put_rows(start, top, a)
         put_rows(recip, low, a)
         put_rows(first, [x * y * F32(1.0 / CENTRE) for x, y in zip(top, low)], a)
@@ -227,88 +267,76 @@
         flux = [geo_a[a, here, :] * grad[a] for a in range(NODES)]
         message[1, here, :] = combine(DERIV[:, 0], flux)
     put_rows(message, rows_of(load, 0), 0)
-    put_rows(message, [lead[pl.ds(8 * b, 8), :] for b in range(NODES)], 2)
+    put_rows(message, rows_of(lead), 2)
     put_rows(message, rows_of(geo_b, 0), 3)
     put_rows(message, rows_of(geo_c, 0), 4)
 
 
-def middle(both, geo_a, geo_b, geo_c, mass, recip_in, first_in, slope, start0, recip0, first0, local, precond, message, work):
+def improve(first, image, recip):
+    return [u * F32(KEEP) + q * d * F32(PULL) for u, q, d in zip(first, image, recip)]
+
+
+def middle(both, geo_a, geo_b, geo_c, mass, recip, first, slope, start0, precond, ahead, message, keep, local, work):
     shared = Shared()
-
-    def summed(which):
-        return [x + y for x, y in zip(rows_of(both, 0, which), rows_of(both, 1, which))]
-
-    lead, fac_b, fac_c = summed(2), summed(3), summed(4)
-    put_rows(work, square_back(fac_c), 0)
-    low = [x + y + z for x, y, z in zip(square_back(fac_b), turned(work, 0), lead)]
-    low = [1.0 / v for v in shared.plane(low)]
-    top = shared.plane(summed(0))
-    head = [x * y * F32(1.0 / CENTRE) for x, y in zip(top, low)]
+    lead, fac_b, fac_c = summed(both, 2), summed(both, 3), summed(both, 4)
+    top, low, head = settle(shared, summed(both, 0), lead, fac_b, fac_c, work.at[0])
     put_rows(start0, top)
-    put_rows(recip0, low)
-    put_rows(first0, head)
-    put_rows(work, stiff_line(turned(first0), fac_c), 0)
-    turn = turned(work, 0)
-    part = stiff_line(head, fac_b)
-    image = [r + k * u + x + y for r, k, u, x, y in zip(summed(1), lead, head, part, turn)]
-    image = shared.plane(image)
-    put_rows(precond, [u * F32(KEEP) + q * d * F32(PULL) for u, q, d in zip(head, image, low)], 0)
-
+    image = within(head, lead, fac_b, fac_c, keep, work.at[0])
+    image = shared.plane([x + y for x, y in zip(summed(both, 1), image)])
+    put_rows(precond, improve(head, image, low), 0)
     for b in range(NODES):
         here = pl.ds(8 * b, 8)
         flux = []
         for a in range(NODES):
             flux.append(geo_a[a, here, :] * (slope[a, here, :] + head[b] * F32(DERIV[a, 0])))
         back = derive_back(flux)
-        for a in range(1, NODES):
+        for a in range(1, NODES - 1):
             local[a, here, :] = back[a]
-    for a in range(1, NODES):
-        put_rows(work, stiff_line(turned(first_in, a), rows_of(geo_c, a)), a)
-    for a in range(1, NODES):
-        values = rows_of(first_in, a)
+        message[0, here, :] = back[NODES - 1]
+    for a in range(1, NODES - 1):
+        put_rows(work, stiff_line(turned(first, a), rows_of(geo_c, a)), a)
+    for a in range(1, NODES - 1):
+        values = rows_of(first, a)
         part = stiff_line(values, rows_of(geo_b, a))
         turn = turned(work, a)
         image = [
             x + y + z + m * v
             for x, y, z, m, v in zip(rows_of(local, a), part, turn, rows_of(mass, a), values)
         ]
-        if a == NODES - 1:
-            put_rows(message, image)
-        else:
-            image = shared.plane(image)
-            low = rows_of(recip_in, a)
-            put_rows(
-                precond,
-                [u * F32(KEEP) + q * d * F32(PULL) for u, q, d in zip(values, image, low)],
-                a,
-            )
-
-
-def finish(pair, geo_a, geo_b, geo_c, mass, load, recip_in, first_in, precond_in, last, image, outer, inner, row, local, work):
-    shared = Shared()
-    whole = shared.plane([x + y for x, y in zip(rows_of(pair, 0), rows_of(pair, 1))])
-    end = [
-        u * F32(KEEP) + q * d * F32(PULL)
-        for u, q, d in zip(rows_of(first_in, NODES - 1), whole, rows_of(recip_in, NODES - 1))
-    ]
-    put_rows(last, end)
-
-    def iterate(a):
-        return rows_of(last) if a == NODES - 1 else rows_of(precond_in, a)
-
+        put_rows(precond, improve(values, shared.plane(image), rows_of(recip, a)), a)
     for b in range(NODES):
         here = pl.ds(8 * b, 8)
-        values = [precond_in[a, here, :] for a in range(NODES - 1)] + [end[b]]
-        back = stiff_line(values, [geo_a[a, here, :] for a in range(NODES)])
+        zero = jnp.zeros((8, 128), F32)
+        grad = derive([precond[a, here, :] for a in range(NODES - 1)] + [zero])
+        for a in range(NODES):
+            ahead[a, here, :] = grad[a]
+        flux = [geo_a[a, here, :] * grad[a] for a in range(NODES)]
+        message[1, here, :] = combine(DERIV[:, NODES - 1], flux)
+
+
+def finish(pair, end, geo_a, geo_b, geo_c, mass, load, recip, first, precond_in, ahead, precond, image, outer, row, keep, local, work):
+    shared = Shared()
+    whole = shared.plane([x + y for x, y in zip(summed(pair, 0), rows_of(end, 3))])
+    tail = improve(rows_of(first, NODES - 1), whole, rows_of(recip, NODES - 1))
+    put_rows(precond, tail)
+    inside = within(tail, rows_of(end, 0), rows_of(end, 1), rows_of(end, 2), keep, work.at[0])
+    put_rows(image, shared.plane([x + y for x, y in zip(summed(pair, 1), inside)]), NODES - 1)
+    for b in range(NODES):
+        here = pl.ds(8 * b, 8)
+        flux = []
+        for a in range(NODES):
+            step = tail[b] * F32(DERIV[a, NODES - 1]) if DERIV[a, NODES - 1] else None
+            flux.append(geo_a[a, here, :] * (ahead[a, here, :] + step))
+        back = derive_back(flux)
         for a in range(NODES):
             local[a, here, :] = back[a]
     for a in range(NODES):
-        lines = turned(last) if a == NODES - 1 else turned(precond_in, a)
+        lines = turned(precond) if a == NODES - 1 else turned(precond_in, a)
         put_rows(work, stiff_line(lines, rows_of(geo_c, a)), a)
     over = [jnp.zeros((8, 128), F32) for _ in range(NODES)]
     under = [jnp.zeros((8, 128), F32) for _ in range(NODES)]
     for a in range(NODES):
-        values = iterate(a)
+        values = tail if a == NODES - 1 else rows_of(precond_in, a)
         part = stiff_line(values, rows_of(geo_b, a))
         turn = turned(work, a)
         total = [
@@ -319,9 +347,7 @@
         under = [s + v * t for s, v, t in zip(under, values, total)]
         if a == 0:
             put_rows(outer, total)
-        elif a == NODES - 1:
-            put_rows(inner, total)
-        else:
+        elif a < NODES - 1:
             put_rows(image, shared.plane(total), a)
     over = jnp.sum(functools.reduce(jnp.add, over), axis=0, keepdims=True)
     under = jnp.sum(functools.reduce(jnp.add, under), axis=0, keepdims=True)
@@ -331,16 +357,20 @@
     row[...] = jnp.broadcast_to(jnp.where(lane < 64, over, under), row.shape)
 
 
-def close(core_ref, order_ref, sums, outer, outer_other, pair, start_in, start0, precond_in, last, image_in, solution_out, residual_out, buf_s, buf_r, sems):
-    shared = Shared()
-    core = core_ref[0]
-    index = jnp.broadcast_to(order_ref[...], (8, CELLS))
+def step_length(sums, alpha):
     lane = lax.broadcasted_iota(jnp.int32, (1, 128), 1)
     total = jnp.sum(sums[...], axis=0, keepdims=True)
     zero = jnp.zeros_like(total)
     over = jnp.sum(jnp.where(lane < 64, total, zero), axis=1, keepdims=True)
     under = jnp.sum(jnp.where(lane < 64, zero, total), axis=1, keepdims=True)
-    alpha = jnp.broadcast_to(over / under, (8, 128))
+    alpha[...] = jnp.broadcast_to(over / under, (8, 128))
+
+
+def close(order_ref, alpha_ref, outer, outer_other, start_in, start0, precond_in, last, image_in, solution_out, residual_out, buf_s, buf_r, sems):
+    shared = Shared()
+    core = lax.axis_index("core")
+    index = jnp.broadcast_to(order_ref[...], (8, CELLS))
+    alpha = alpha_ref[...]
     at = [a + core * (NODES - 1 - 2 * a) for a in range(NODES)]
     copies = []
     for a in range(NODES):
@@ -348,12 +378,12 @@
             head, values = rows_of(start0), rows_of(precond_in, 0)
             image = shared.plane([x + y for x, y in zip(rows_of(outer), rows_of(outer_other))])
         elif a == NODES - 1:
-            head, values = rows_of(start_in, a), rows_of(last)
-            image = shared.plane([x + y for x, y in zip(rows_of(pair, 0), rows_of(pair, 1))])
+            head, values, image = rows_of(start_in, a), rows_of(last), rows_of(image_in, a)
         else:
             head, values, image = rows_of(start_in, a), rows_of(precond_in, a), rows_of(image_in, a)
-        put_rows(buf_s, [lanes_of(alpha * v, index) for v in values], a)
-        put_rows(buf_r, [lanes_of(s - alpha * i, index) for s, i in zip(head, image)], a)
+        for b, (v, s, i) in enumerate(zip(values, head, image)):
+            buf_s[a, b] = lanes_of(alpha * v, index)
+            buf_r[a, b] = lanes_of(s - alpha * i, index)
         for i, (buf, out) in enumerate(((buf_s, solution_out), (buf_r, residual_out))):
             copy = pltpu.make_async_copy(buf.at[a], out.at[at[a]], sems.at[i, a])
             copy.start()
@@ -362,18 +392,22 @@
         copy.wait()
 
 
+def gather_up(sums, row):
+    row[...] = jnp.broadcast_to(jnp.sum(sums[...], axis=0, keepdims=True), row.shape)
+
+
 VMEM = pl.BlockSpec(memory_space=pltpu.VMEM)
-SMEM = pl.BlockSpec(memory_space=pltpu.SMEM)
+HBM = pl.BlockSpec(memory_space=pltpu.HBM)
 ANY = pl.BlockSpec(memory_space=pl.ANY)
 FIELD = (NODES, 64, 128)
 FACE = (64, 128)
-
-
-def call(body, name, outs, ins, scratch=(), out_specs=None, flops=4_000_000):
+BLOCK = (NODES, NODES, NODES, CELLS)
+
+
+def call(body, outs, ins, scratch=(), out_specs=None, flops=4_000_000):
     return pl.pallas_call(
         body,
-        name=name,
-        out_shape=[jax.ShapeDtypeStruct(s, F32) for s in outs],
+        out_shape=[jax.ShapeDtypeStruct(s, F32) if isinstance(s, tuple) else s for s in outs],
         in_specs=ins,
         out_specs=out_specs or [VMEM] * len(outs),
         scratch_shapes=list(scratch),
@@ -387,58 +421,55 @@
     for axis in AXES:
         count *= lax.axis_size(axis)
     across_chips = [[2 * k + 1, (2 * k + 2) % count] for k in range(count // 2)]
+    plane_groups, line_groups = groups((1, 3)), groups((0, 2))
+    in_chip = [[2 * k + 1, 2 * k] for k in range(count // 2)]
     swap = [(i, (i + 1) % count if i % 2 else (i - 1) % count) for i in range(count)]
-    core = lax.axis_index("core").astype(jnp.int32).reshape(1)
-    field = jax.ShapeDtypeStruct(FIELD, F32)
     dma = pltpu.SemaphoreType.DMA
-    load_terms = load_terms.reshape(FIELD)
-    geometry = geometry.reshape(3, *FIELD)
-    mass_terms = mass_terms.reshape(FIELD)
-
-    load, geo_a, geo_b, geo_c, mass, diag, lead, message = call(
+    arguments = (
+        element_order,
+        load_terms.reshape(FIELD),
+        geometry.reshape(3, *FIELD),
+        mass_terms.reshape(FIELD),
+    )
+    arguments = [pltpu.with_memory_space_constraint(x, pltpu.HBM) for x in arguments]
+
+    load, geo_a, geo_b, geo_c, mass, diag, lead, message, order = call(
         prepare,
-        "prepare",
-        [FIELD] * 6 + [FACE, (2, *FACE)],
-        [SMEM, VMEM, ANY, ANY, ANY],
-        [pltpu.VMEM((5, *FIELD), F32), dma((5,))],
-    )(core, element_order, load_terms, geometry, mass_terms)
-    pair = lax.all_gather(message, "core")
-    start, recip, first, slope, message = call(
-        begin, "begin", [FIELD] * 4 + [(5, *FACE)], [VMEM] * 7
+        [FIELD] * 6 + [FACE, (5, *FACE), jax.ShapeDtypeStruct((1, CELLS), jnp.int32)],
+        [HBM] * 4,
+        [pltpu.VMEM((5, *FIELD), F32), dma((6,))],
+    )(*arguments)
+    pair = lax.all_gather(message, AXES, axis_index_groups=in_chip)
+    start, recip, first, slope, message, end = call(
+        begin, [FIELD] * 4 + [(5, *FACE), (4, *FACE)], [VMEM] * 7, [pltpu.VMEM(FACE, F32), pltpu.VMEM(FACE, F32)]
     )(load, geo_a, geo_b, geo_c, diag, lead, pair)
     both = lax.all_gather(message, AXES, axis_index_groups=across_chips)
-    start0, recip0, first0, local, precond, message = call(
+    start0, precond, ahead, message = call(
         middle,
-        "middle",
-        [FACE] * 3 + [FIELD, FIELD, FACE],
+        [FACE, FIELD, FIELD, (2, *FACE)],
         [VMEM] * 8,
-        [pltpu.VMEM(FIELD, F32)],
+        [pltpu.VMEM(FACE, F32), pltpu.VMEM(FIELD, F32), pltpu.VMEM(FIELD, F32)],
     )(both, geo_a, geo_b, geo_c, mass, recip, first, slope)
-    pair = lax.all_gather(message, "core")
-    group = lax.axis_size("ty") * lax.axis_size("tx")
-    last, image, outer, inner, row = call(
+    pair = lax.all_gather(message, AXES, axis_index_groups=in_chip)
+    last, image, outer, row = call(
         finish,
-        "finish",
-        [FACE, FIELD, FACE, FACE, (group, 128)],
-        [VMEM] * 9,
-        [pltpu.VMEM(FIELD, F32), pltpu.VMEM(FIELD, F32)],
-    )(pair, geo_a, geo_b, geo_c, mass, load, recip, first, precond)
+        [FACE, FIELD, FACE, (len(plane_groups[0]), 128)],
+        [VMEM] * 11,
+        [pltpu.VMEM(FACE, F32), pltpu.VMEM(FIELD, F32), pltpu.VMEM(FIELD, F32)],
+    )(pair, end, geo_a, geo_b, geo_c, mass, load, recip, first, precond, ahead)
     outer_other = lax.ppermute(outer, AXES, swap)
-    pair = lax.all_gather(inner, "core")
-    sums = lax.all_to_all(row, ("ty", "tx"), 0, 0, tiled=True)
-    group = lax.axis_size("tz") * lax.axis_size("core")
-    row = jnp.broadcast_to(jnp.sum(sums, axis=0, keepdims=True), (group, 128))
-    sums = lax.all_to_all(row, ("tz", "core"), 0, 0, tiled=True)
+    sums = lax.all_to_all(row, AXES, 0, 0, tiled=True, axis_index_groups=plane_groups)
+    (row,) = call(gather_up, [(len(line_groups[0]), 128)], [VMEM], flops=100_000)(sums)
+    sums = lax.all_to_all(row, AXES, 0, 0, tiled=True, axis_index_groups=line_groups)
+    (alpha,) = call(step_length, [(8, 128)], [VMEM], flops=100_000)(sums)
     solution, residual = call(
         close,
-        "close",
-        [FIELD, FIELD],
-        [SMEM] + [VMEM] * 10,
-        [pltpu.VMEM(FIELD, F32), pltpu.VMEM(FIELD, F32), dma((2, NODES))],
+        [BLOCK, BLOCK],
+        [VMEM] * 9,
+        [pltpu.VMEM(BLOCK, F32), pltpu.VMEM(BLOCK, F32), dma((2, NODES))],
         out_specs=[ANY, ANY],
-    )(core, element_order, sums, outer, outer_other, pair, start, start0, precond, last, image)
-    shape = (NODES, NODES, NODES, CELLS)
-    return solution.reshape(shape), residual.reshape(shape)
+    )(order, alpha, outer, outer_other, start, start0, precond, last, image)
+    return solution, residual
 
 
 def solution(mesh):

time: 68.1 us -> 58.2 us (0.85)
  starting transfers between devices: 11.7 us -> 7.08 us
  blocking collectives: 43.6 us -> 39 us
  local copies, waits for them, and re-layouts: 4.29 us -> 0 us
  waiting for transfers between devices: 2.3 us -> 4.83 us
    all_gather x3 -> x2, blocking collectives: 25.4 us -> 20.8 us  [on_device(): pair = lax.all_gather(message, AXES, axis_index_groups=in_chip)]
    all_to_all x1, starting transfers between devices: 9.42 us -> 5.16 us  [on_device(): lax.all_to_all(row, AXES, 0, 0, tiled=True, axis_index_groups=plane_groups)]
    unnamed x8 -> x0, local copies, waits for them, and re-layouts: 3.68 us -> none
    all_to_all x1, waiting for transfers between devices: 2.3 us -> 4.83 us  [on_device(): lax.all_to_all(row, AXES, 0, 0, tiled=True, axis_index_groups=plane_groups)]
    pallas_call x5 -> x7, Pallas kernels: 5.11 us -> 5.75 us  [the longest x1 1.81 us: on_device(): call(prepare, [FIELD] * 6 + [FACE, (5, *FACE), jax.ShapeDtypeStruct((1, C...]
where the time goes in v2:
time: 58.2 us; the launch traced here: 57.4 us
  blocking collectives  39 us (67%)
  starting transfers between devices  7.08 us (12%)
  Pallas kernels  5.75 us (10%)
  waiting for transfers between devices  4.83 us (8%)
  between operations  0.66 us (1%)
    all_gather x2, blocking collectives, on_device(): pair = lax.all_gather(message, AXES, axis_index_groups=in_chip)  20.8 us
    all_to_all x1, blocking collectives, on_device(): lax.all_to_all(row, AXES, 0, 0, tiled=True, axis_index_groups=line_groups)  12.8 us
    all_gather x1, blocking collectives, on_device(): both = lax.all_gather(message, AXES, axis_index_groups=across_chips)  5.43 us
    all_to_all x1, starting transfers between devices, on_device(): lax.all_to_all(row, AXES, 0, 0, tiled=True, axis_index_groups=plane_groups)  5.16 us
    all_to_all x1, waiting for transfers between devices, on_device(): lax.all_to_all(row, AXES, 0, 0, tiled=True, axis_index_groups=plane_groups)  4.83 us
    ppermute x1, starting transfers between devices, on_device(): outer_other = lax.ppermute(outer, AXES, swap)  1.92 us
    pallas_call x1, Pallas kernels, on_device(): call(prepare, [FIELD] * 6 + [FACE, (5, *FACE), jax.ShapeDtypeStruct((1, C...  1.81 us
    pallas_call x1, Pallas kernels, on_device(): call(finish, [FACE, FIELD, FACE, (len(plane_groups[0]), 128)], [VMEM] * 1...  1.35 us
  transfers between devices with their start and end apart: 2, of which 1 were waited for; matrix products, arithmetic and copies ran while one was open for 0% of the time, Pallas kernels for 0%

profile of v2, /device:TPU:1, one launch (start us, length us, event | category | flops | bytes accessed | tf_op | source)
XLA Modules:
  0.0 57.4 jit_solution(10092881920860443221)
XLA Ops:
  0.6 1.8 %shard_map.59 = (f32[8,64,128]{2,1,0:T(8,128)S(1)}, f32[8,64,128]{2,1,0:T(8,128)S(1)}, f32[8,64,128]{2,1,0:T(8,128)S(1)}, f32[8,64,128]{2,1,0:T(8,128)S(1)}, f32...) custom-call(s32[1,128]{1,0:T(1,128)} %order_in.1, ...), custom_call_target="tpu_custom_call" | custom-call | flops 4000000 | bytes 2097152 | tf_op jit(solution)/shard_map/pallas_call | solution.py:436
  2.4 12.1 %all-gather = f32[10,64,128]{2,1,0:T(8,128)S(1)} all-gather(f32[5,64,128]{2,1,0:T(8,128)S(1)} %get-tuple-element.32), channel_id=2, replica_groups={{1,0},{3,2},{5,4},{7,6},{9,8},{11,10},{13,12},{15,14},{17,16},{19,18},{..., dimensions={0}, use_global_device_ids=true | all-gather | bytes 491520 | tf_op jit(solution)/shard_map/all_gather | solution.py:442
  14.6 0.6 %shard_map.60 = (f32[8,64,128]{2,1,0:T(8,128)S(1)}, f32[8,64,128]{2,1,0:T(8,128)S(1)}, f32[8,64,128]{2,1,0:T(8,128)S(1)}, f32[8,64,128]{2,1,0:T(8,128)S(1)}, f32...) custom-call(f32[8,64,128]{2,1,0:T(8,128)S(1)} %get-tuple-element.26.load, f32[8,64,128]{2,1,0:T(8,128)S(1)} %get-tuple-element.27.geo_a, ...), custom_call_target="tpu_custom_call" | custom-call | flops 4000000 | bytes 2097152 | tf_op jit(solution)/shard_map/pallas_call | solution.py:443
  15.2 5.4 %all-gather.1 = f32[10,64,128]{2,1,0:T(8,128)S(1)} all-gather(f32[5,64,128]{2,1,0:T(8,128)S(1)} %get-tuple-element.33), channel_id=3, replica_groups={{1,2},{3,4},{5,6},{7,8},{9,10},{11,12},{13,14},{15,16},{17,18},{19,20},..., dimensions={0}, use_global_device_ids=true | all-gather | bytes 491520 | tf_op jit(solution)/shard_map/all_gather | solution.py:446
  20.6 0.7 %shard_map.61 = (f32[64,128]{1,0:T(8,128)S(1)}, f32[8,64,128]{2,1,0:T(8,128)S(1)}, f32[8,64,128]{2,1,0:T(8,128)S(1)}, f32[2,64,128]{2,1,0:T(8,128)S(1)}) custom-call(f32[2,5,64,128]{3,2,1,0:T(8,128)S(1)} %bitcast.15, f32[8,64,128]{2,1,0:T(8,128)S(1)} %get-tuple-element.27.geo_a, f32[8,64,128]{2,1,0:T(8,128)S(1)} %get-tuple-element.28.geo_b, ...), custom_call_target="tpu_custom_call" | custom-call | flops 4000000 | bytes 2097152 | tf_op jit(solution)/shard_map/pallas_call | solution.py:447
  21.3 8.7 %all-gather.2 = f32[4,64,128]{2,1,0:T(8,128)S(1)} all-gather(f32[2,64,128]{2,1,0:T(8,128)S(1)} %get-tuple-element.38), channel_id=4, replica_groups={{1,0},{3,2},{5,4},{7,6},{9,8},{11,10},{13,12},{15,14},{17,16},{19,18},{..., dimensions={0}, use_global_device_ids=true | all-gather | bytes 196608 | tf_op jit(solution)/shard_map/all_gather | solution.py:453
  30.0 1.4 %shard_map.62 = (f32[64,128]{1,0:T(8,128)S(1)}, f32[8,64,128]{2,1,0:T(8,128)S(1)}, f32[64,128]{1,0:T(8,128)S(1)}, f32[24,128]{1,0:T(8,128)}) custom-call(f32[2,2,64,128]{3,2,1,0:T(8,128)S(1)} %bitcast.16, f32[4,64,128]{2,1,0:T(8,128)S(1)} %get-tuple-element.39.end, f32[8,64,128]{2,1,0:T(8,128)S(1)} %get-tuple-element.27.geo_a, ...), custom_call_target="tpu_custom_call" | custom-call | flops 4000000 | bytes 2097152 | tf_op jit(solution)/shard_map/pallas_call | solution.py:454
  31.4 5.2 %all-to-all-start = ((f32[24,1,128]{2,1,0:T(1,128)}), f32[24,1,128]{2,1,0:T(1,128)S(1)}, u32[]{:S(2)}, u32[]{:S(2)}) async-start(f32[24,1,128]{2,1,0:T(1,128)} %bitcast.7), calls=%async_computation | async-start | bytes 24576 | tf_op jit(solution)/shard_map/all_to_all | solution.py:461
  36.5 1.9 %collective-permute-start = (f32[64,128]{1,0:T(8,128)S(1)}, f32[64,128]{1,0:T(8,128)S(1)}, u32[]{:S(2)}, u32[]{:S(2)}) collective-permute-start(f32[64,128]{1,0:T(8,128)S(1)} %get-tuple-element.43.outer), channel_id=1, source_target_pairs={{0,767},{1,2},{2,1},{3,4},{4,3},{5,6},{6,5},{7,8},{8,7},{9,10},{10... | collective-permute-start | bytes 98312 | tf_op jit(solution)/shard_map/ppermute | solution.py:460
  38.5 4.8 %all-to-all-done = f32[24,1,128]{2,1,0:T(1,128)S(1)} async-done(((f32[24,1,128]{2,1,0:T(1,128)}), f32[24,1,128]{2,1,0:T(1,128)S(1)}, u32[]{:S(2)}, u32[]{:S(2)}) %all-to-all-start) | async-done | bytes 12320 | tf_op jit(solution)/shard_map/all_to_all | solution.py:461
  43.3 12.8 %all_to_all.22 = f32[32,1,128]{2,1,0:T(1,128)S(1)} all-to-all(f32[32,1,128]{2,1,0:T(1,128)S(1)} %bitcast.17), channel_id=1, replica_groups={{661,663,657,659,757,759,753,755,85,87,81,83,181,183,177,179,277,279,27..., dimensions={0} | all-to-all | bytes 32768 | tf_op jit(solution)/shard_map/all_to_all | solution.py:463
  56.1 0.1 shard_map.64.alpha_ref
  56.2 0.0 collective-permute-done.outer_other
  56.2 1.2 %shard_map.65 = (f32[8,8,8,128]{3,2,1,0:T(8,128)}, f32[8,8,8,128]{3,2,1,0:T(8,128)}) custom-call(s32[1,128]{1,0:T(1,128)S(1)} %get-tuple-element.25.order_ref, f32[8,128]{1,0:T(8,128)S(1)} %shard_map.64.alpha_ref, f32[64,128]{1,0:T(8,128)S(1)} %get-tuple-element.43.outer, f32[64,128]{1,0:T(8,128)S(1)} %collective-permute-done.outer_other, ...), custom_call_target="tpu_custom_call" | custom-call | flops 4000000 | bytes 2097152 | tf_op jit(solution)/shard_map/pallas_call | solution.py:465
  (1 shorter events, 0.0 us)
Async XLA Ops:
  31.4 11.9 %all-to-all-start = ((f32[24,1,128]{2,1,0:T(1,128)}), f32[24,1,128]{2,1,0:T(1,128)S(1)}, u32[]{:S(2)}, u32[]{:S(2)}) async-start(f32[24,1,128]{2,1,0:T(1,128)} %bitcast.7), calls=%async_computation | async-start | bytes 24576 | tf_op jit(solution)/shard_map/all_to_all | solution.py:461
  36.5 19.6 %collective-permute-start = (f32[64,128]{1,0:T(8,128)S(1)}, f32[64,128]{1,0:T(8,128)S(1)}, u32[]{:S(2)}, u32[]{:S(2)}) collective-permute-start(f32[64,128]{1,0:T(8,128)S(1)} %get-tuple-element.43.outer), channel_id=1, source_target_pairs={{0,767},{1,2},{2,1},{3,4},{4,3},{5,6},{6,5},{7,8},{8,7},{9,10},{10... | collective-permute-start | bytes 98312 | tf_op jit(solution)/shard_map/ppermute | solution.py:460

commit v3 on v2

--- a/solution.py
+++ b/solution.py
@@ -12,7 +12,7 @@
 
 TORUS = (8, 12, 4, 2)
 AXES = ("ty", "tz", "tx", "core")
-ROOT = (6, 10, 2, 1)
+ROOT = (5, 10, 3, 1)
 
 
 def groups(axes):
@@ -169,56 +169,66 @@
     return [ref[(*at, pl.ds(c, 8, stride=8), slice(None))] for c in range(NODES)]
 
 
-def prepare(order_in, load_in, geom_in, mass_in, load, geo_a, geo_b, geo_c, mass, diag, lead, message, order_ref, raw, sems):
+def mirrored():
+    core = lax.axis_index("core")
+    return [a + core * (NODES - 1 - 2 * a) for a in range(NODES)]
+
+
+def prepare(order_in, load_in, geom_in, mass_in, load, geo_a, geo_b, geo_c, mass, diag, lead, message, order_ref, raw, work, index_ref, sems):
     order_copy = pltpu.make_async_copy(order_in, order_ref, sems.at[5])
     order_copy.start()
     sources = [geom_in.at[0], geom_in.at[1], geom_in.at[2], mass_in, load_in]
     copies = [pltpu.make_async_copy(src, raw.at[i], sems.at[i]) for i, src in enumerate(sources)]
     for copy in copies:
         copy.start()
-    core = lax.axis_index("core")
-    order_copy.wait()
-    cells = jnp.broadcast_to(order_ref[...], (CELLS, CELLS))
-    hot = (cells == lax.broadcasted_iota(jnp.int32, (CELLS, CELLS), 0)).astype(F32)
-    column = lax.broadcasted_iota(jnp.int32, (8, CELLS), 1).astype(F32)
-    index = lax.dot_general(column, hot, (((1,), (1,)), ((), ())), preferred_element_type=F32)
-    index = index.astype(jnp.int32)
-    at = [a + core * (NODES - 1 - 2 * a) for a in range(NODES)]
+
+    @pl.when(lax.axis_index("core") >= 0)
+    def invert():
+        order_copy.wait()
+        cells = jnp.broadcast_to(order_ref[...], (CELLS, CELLS))
+        hot = (cells == lax.broadcasted_iota(jnp.int32, (CELLS, CELLS), 0)).astype(F32)
+        column = lax.broadcasted_iota(jnp.int32, (8, CELLS), 1).astype(F32)
+        index = lax.dot_general(column, hot, (((1,), (1,)), ((), ())), preferred_element_type=F32)
+        index_ref[...] = index.astype(jnp.int32)
+
+    at = mirrored()
+    for copy in copies:
+        copy.wait()
+    index = index_ref[...]
 
     def fetch(which, a):
         return [lanes_of(v, index) for v in rows_of(raw, which, at[a])]
 
-    copies[0].wait()
-    for a in range(NODES):
-        put_rows(geo_a, fetch(0, a), a)
-    copies[1].wait()
-    for a in range(NODES):
-        put_rows(geo_b, fetch(1, a), a)
-    copies[2].wait()
-    for a in range(NODES):
-        for c in range(NODES):
-            geo_c[a, pl.ds(8 * c, 8), :] = lanes_of(raw[2, at[a], pl.ds(c, 8, stride=8), :], index)
-    copies[3].wait()
-    for a in range(NODES):
-        put_rows(mass, fetch(3, a), a)
-    copies[4].wait()
-    for a in range(NODES):
-        put_rows(load, fetch(4, a), a)
-    for a in range(1, NODES - 1):
-        put_rows(diag, square_back(rows_of(geo_c, a)), a)
-    for a in range(1, NODES - 1):
-        part = square_back(rows_of(geo_b, a))
-        turn = turned(diag, a)
-        put_rows(diag, [x + y + z for x, y, z in zip(part, turn, rows_of(mass, a))], a)
     for b in range(NODES):
         here = pl.ds(8 * b, 8)
-        part = square_back([geo_a[a, here, :] for a in range(NODES)])
-        lead[here, :] = part[0] + mass[0, here, :]
+        lines = [lanes_of(raw[0, at[a], here, :], index) for a in range(NODES)]
+        part = square_back(lines)
+        for a in range(NODES):
+            geo_a[a, here, :] = lines[a]
+        lead[here, :] = part[0]
         for a in range(1, NODES - 1):
-            diag[a, here, :] = diag[a, here, :] + part[a]
+            diag[a, here, :] = part[a]
         message[1, here, :] = part[NODES - 1]
-    for i, ref in ((0, load), (2, mass), (3, geo_b), (4, geo_c)):
-        put_rows(message, rows_of(ref, NODES - 1), i)
+    for a in range(NODES):
+        lines = [lanes_of(v, index) for v in turned(raw, 2, at[a])]
+        put_rows(geo_c, lines, a)
+        if 0 < a < NODES - 1:
+            put_rows(work, square_back(lines), a)
+        elif a == NODES - 1:
+            put_rows(message, lines, 4)
+    for a in range(NODES):
+        lines, weights, values = fetch(1, a), fetch(3, a), fetch(4, a)
+        put_rows(geo_b, lines, a)
+        put_rows(mass, weights, a)
+        put_rows(load, values, a)
+        if a == 0:
+            put_rows(lead, [x + y for x, y in zip(rows_of(lead), weights)])
+        elif a == NODES - 1:
+            for i, rows in ((0, values), (2, weights), (3, lines)):
+                put_rows(message, rows, i)
+        else:
+            parts = square_back(lines), turned(work, a), weights, rows_of(diag, a)
+            put_rows(diag, [w + x + y + z for w, x, y, z in zip(*parts)], a)
 
 
 def summed(ref, which):
@@ -314,47 +324,84 @@
         message[1, here, :] = combine(DERIV[:, NODES - 1], flux)
 
 
-def finish(pair, end, geo_a, geo_b, geo_c, mass, load, recip, first, precond_in, ahead, precond, image, outer, row, keep, local, work):
+def finish(pair, end, geo_a, geo_b, geo_c, mass, load, recip, first, precond_in, ahead, precond, image, outer, row, keep, flux_a, flux_b, flux_c, row_buf, row_sem):
     shared = Shared()
     whole = shared.plane([x + y for x, y in zip(summed(pair, 0), rows_of(end, 3))])
     tail = improve(rows_of(first, NODES - 1), whole, rows_of(recip, NODES - 1))
     put_rows(precond, tail)
-    inside = within(tail, rows_of(end, 0), rows_of(end, 1), rows_of(end, 2), keep, work.at[0])
-    put_rows(image, shared.plane([x + y for x, y in zip(summed(pair, 1), inside)]), NODES - 1)
+
+    def iterate(a):
+        return tail if a == NODES - 1 else rows_of(precond_in, a)
+
+    over = [jnp.zeros((8, 128), F32) for _ in range(NODES)]
+    under = [jnp.zeros((8, 128), F32) for _ in range(NODES)]
     for b in range(NODES):
         here = pl.ds(8 * b, 8)
-        flux = []
         for a in range(NODES):
-            step = tail[b] * F32(DERIV[a, NODES - 1]) if DERIV[a, NODES - 1] else None
-            flux.append(geo_a[a, here, :] * (ahead[a, here, :] + step))
-        back = derive_back(flux)
-        for a in range(NODES):
-            local[a, here, :] = back[a]
+            grad = ahead[a, here, :] + tail[b] * F32(DERIV[a, NODES - 1])
+            flux = geo_a[a, here, :] * grad
+            flux_a[a, here, :] = flux
+            under[a] = under[a] + flux * grad
     for a in range(NODES):
-        lines = turned(precond) if a == NODES - 1 else turned(precond_in, a)
-        put_rows(work, stiff_line(lines, rows_of(geo_c, a)), a)
-    over = [jnp.zeros((8, 128), F32) for _ in range(NODES)]
-    under = [jnp.zeros((8, 128), F32) for _ in range(NODES)]
+        grad = derive(turned(precond) if a == NODES - 1 else turned(precond_in, a))
+        flux = [g * d for g, d in zip(rows_of(geo_c, a), grad)]
+        put_rows(flux_c, flux, a)
+        under = [s + f * d for s, f, d in zip(under, flux, grad)]
     for a in range(NODES):
-        values = tail if a == NODES - 1 else rows_of(precond_in, a)
-        part = stiff_line(values, rows_of(geo_b, a))
-        turn = turned(work, a)
-        total = [
-            x + y + z + m * v
-            for x, y, z, m, v in zip(rows_of(local, a), part, turn, rows_of(mass, a), values)
-        ]
-        over = [s + v * f for s, v, f in zip(over, values, rows_of(load, a))]
-        under = [s + v * t for s, v, t in zip(under, values, total)]
-        if a == 0:
-            put_rows(outer, total)
-        elif a < NODES - 1:
-            put_rows(image, shared.plane(total), a)
+        values = iterate(a)
+        grad = derive(values)
+        flux = [g * d for g, d in zip(rows_of(geo_b, a), grad)]
+        put_rows(flux_b, flux, a)
+        under = [s + f * d for s, f, d in zip(under, flux, grad)]
+        under = [s + m * v * v for s, m, v in zip(under, rows_of(mass, a), values)]
+        over = [s + f * v for s, f, v in zip(over, rows_of(load, a), values)]
     over = jnp.sum(functools.reduce(jnp.add, over), axis=0, keepdims=True)
     under = jnp.sum(functools.reduce(jnp.add, under), axis=0, keepdims=True)
     over = over + pltpu.roll(over, 64, 1)
     under = under + pltpu.roll(under, 64, 1)
     lane = lax.broadcasted_iota(jnp.int32, (1, 128), 1)
-    row[...] = jnp.broadcast_to(jnp.where(lane < 64, over, under), row.shape)
+    row_buf[...] = jnp.broadcast_to(jnp.where(lane < 64, over, under), row_buf.shape)
+    row_copy = pltpu.make_async_copy(row_buf, row, row_sem)
+    row_copy.start()
+
+    @pl.when(lax.axis_index("core") >= 0)
+    def apply():
+        for b in range(NODES):
+            here = pl.ds(8 * b, 8)
+            back = derive_back([flux_a[a, here, :] for a in range(NODES)])
+            for a in range(NODES - 1):
+                flux_a[a, here, :] = back[a]
+        for a in range(NODES - 1):
+            put_rows(flux_c, derive_back(rows_of(flux_c, a)), a)
+        for a in range(NODES - 1):
+            values = rows_of(precond_in, a)
+            part = derive_back(rows_of(flux_b, a))
+            turn = turned(flux_c, a)
+            total = [
+                x + y + z + m * v
+                for x, y, z, m, v in zip(rows_of(flux_a, a), part, turn, rows_of(mass, a), values)
+            ]
+            if a == 0:
+                put_rows(outer, total)
+            else:
+                put_rows(image, Shared().plane(total), a)
+        inside = within(rows_of(precond), rows_of(end, 0), rows_of(end, 1), rows_of(end, 2), keep, flux_c.at[NODES - 1])
+        inside = [x + y for x, y in zip(summed(pair, 1), inside)]
+        put_rows(image, Shared().plane(inside), NODES - 1)
+
+    row_copy.wait()
+
+
+def restore(order_ref, start_in, start0, precond_in, last, image_in, start, precond, image):
+    index = jnp.broadcast_to(order_ref[...], (8, CELLS))
+    for a in range(NODES):
+        for out, rows in (
+            (start, rows_of(start0) if a == 0 else rows_of(start_in, a)),
+            (precond, rows_of(last) if a == NODES - 1 else rows_of(precond_in, a)),
+            (image, None if a == 0 else rows_of(image_in, a)),
+        ):
+            if rows is not None:
+                put_rows(out, [lanes_of(v, index) for v in rows], a)
 
 
 def step_length(sums, alpha):
@@ -366,24 +413,19 @@
     alpha[...] = jnp.broadcast_to(over / under, (8, 128))
 
 
-def close(order_ref, alpha_ref, outer, outer_other, start_in, start0, precond_in, last, image_in, solution_out, residual_out, buf_s, buf_r, sems):
+def close(alpha_ref, order_ref, outer, outer_other, start, precond, image, solution_out, residual_out, buf_s, buf_r, sems):
     shared = Shared()
-    core = lax.axis_index("core")
+    alpha = alpha_ref[...]
     index = jnp.broadcast_to(order_ref[...], (8, CELLS))
-    alpha = alpha_ref[...]
-    at = [a + core * (NODES - 1 - 2 * a) for a in range(NODES)]
+    at = mirrored()
+    head = shared.plane([x + y for x, y in zip(rows_of(outer), rows_of(outer_other))])
+    head = [lanes_of(v, index) for v in head]
     copies = []
-    for a in range(NODES):
-        if a == 0:
-            head, values = rows_of(start0), rows_of(precond_in, 0)
-            image = shared.plane([x + y for x, y in zip(rows_of(outer), rows_of(outer_other))])
-        elif a == NODES - 1:
-            head, values, image = rows_of(start_in, a), rows_of(last), rows_of(image_in, a)
-        else:
-            head, values, image = rows_of(start_in, a), rows_of(precond_in, a), rows_of(image_in, a)
-        for b, (v, s, i) in enumerate(zip(values, head, image)):
-            buf_s[a, b] = lanes_of(alpha * v, index)
-            buf_r[a, b] = lanes_of(s - alpha * i, index)
+    for a in (1, 2, 3, 4, 5, 6, 7, 0):
+        rows = head if a == 0 else rows_of(image, a)
+        for b, (v, s, i) in enumerate(zip(rows_of(precond, a), rows_of(start, a), rows)):
+            buf_s[a, b] = alpha * v
+            buf_r[a, b] = s - alpha * i
         for i, (buf, out) in enumerate(((buf_s, solution_out), (buf_r, residual_out))):
             copy = pltpu.make_async_copy(buf.at[a], out.at[at[a]], sems.at[i, a])
             copy.start()
@@ -421,7 +463,7 @@
     for axis in AXES:
         count *= lax.axis_size(axis)
     across_chips = [[2 * k + 1, (2 * k + 2) % count] for k in range(count // 2)]
-    plane_groups, line_groups = groups((1, 3)), groups((0, 2))
+    first_groups, second_groups = groups((1, 3)), groups((0, 2))
     in_chip = [[2 * k + 1, 2 * k] for k in range(count // 2)]
     swap = [(i, (i + 1) % count if i % 2 else (i - 1) % count) for i in range(count)]
     dma = pltpu.SemaphoreType.DMA
@@ -437,7 +479,12 @@
         prepare,
         [FIELD] * 6 + [FACE, (5, *FACE), jax.ShapeDtypeStruct((1, CELLS), jnp.int32)],
         [HBM] * 4,
-        [pltpu.VMEM((5, *FIELD), F32), dma((6,))],
+        [
+            pltpu.VMEM((5, *FIELD), F32),
+            pltpu.VMEM(FIELD, F32),
+            pltpu.VMEM((8, CELLS), jnp.int32),
+            dma((6,)),
+        ],
     )(*arguments)
     pair = lax.all_gather(message, AXES, axis_index_groups=in_chip)
     start, recip, first, slope, message, end = call(
@@ -453,22 +500,29 @@
     pair = lax.all_gather(message, AXES, axis_index_groups=in_chip)
     last, image, outer, row = call(
         finish,
-        [FACE, FIELD, FACE, (len(plane_groups[0]), 128)],
+        [FACE, FIELD, FACE, (len(first_groups[0]), 128)],
         [VMEM] * 11,
-        [pltpu.VMEM(FACE, F32), pltpu.VMEM(FIELD, F32), pltpu.VMEM(FIELD, F32)],
+        [
+            pltpu.VMEM(FACE, F32),
+            *[pltpu.VMEM(FIELD, F32)] * 3,
+            pltpu.VMEM((len(first_groups[0]), 128), F32),
+            dma,
+        ],
+        out_specs=[VMEM] * 3 + [ANY],
     )(pair, end, geo_a, geo_b, geo_c, mass, load, recip, first, precond, ahead)
     outer_other = lax.ppermute(outer, AXES, swap)
-    sums = lax.all_to_all(row, AXES, 0, 0, tiled=True, axis_index_groups=plane_groups)
-    (row,) = call(gather_up, [(len(line_groups[0]), 128)], [VMEM], flops=100_000)(sums)
-    sums = lax.all_to_all(row, AXES, 0, 0, tiled=True, axis_index_groups=line_groups)
+    sums = lax.all_to_all(row, AXES, 0, 0, tiled=True, axis_index_groups=first_groups)
+    (row,) = call(gather_up, [(len(second_groups[0]), 128)], [VMEM], flops=100_000)(sums)
+    sums = lax.all_to_all(row, AXES, 0, 0, tiled=True, axis_index_groups=second_groups)
     (alpha,) = call(step_length, [(8, 128)], [VMEM], flops=100_000)(sums)
+    start, precond, image = call(restore, [FIELD] * 3, [VMEM] * 6)(order, start, start0, precond, last, image)
     solution, residual = call(
         close,
         [BLOCK, BLOCK],
-        [VMEM] * 9,
+        [VMEM] * 7,
         [pltpu.VMEM(BLOCK, F32), pltpu.VMEM(BLOCK, F32), dma((2, NODES))],
         out_specs=[ANY, ANY],
-    )(order, alpha, outer, outer_other, start, start0, precond, last, image)
+    )(alpha, order, outer, outer_other, start, precond, image)
     return solution, residual
 
 

time: 58.2 us -> 57 us (0.979); the launches traced: 57.4 us -> 56.8 us
  blocking collectives: 39 us -> 26.3 us
  starting transfers between devices: 7.08 us -> 15.9 us
  waiting for transfers between devices: 4.83 us -> 7.79 us
    all_to_all x1 -> x0, blocking collectives: 12.8 us -> none  [on_device(): lax.all_to_all(row, AXES, 0, 0, tiled=True, axis_index_groups=line_groups)]
    all_to_all x1 -> x2, starting transfers between devices: 5.16 us -> 14 us  [the longest x1 8.81 us: on_device(): lax.all_to_all(row, AXES, 0, 0, tiled=True, axis_index_groups=second_groups)]
    all_to_all x1 -> x2, waiting for transfers between devices: 4.83 us -> 7.78 us  [the longest x1 4.83 us: on_device(): lax.all_to_all(row, AXES, 0, 0, tiled=True, axis_index_groups=first_groups)]
    pallas_call x3 -> x4, Pallas kernels: 2.54 us -> 2.96 us  [the longest x1 1.09 us: on_device(): call(finish, [FACE, FIELD, FACE, (len(first_groups[0]), 128)], [VMEM] * 1...]
  transfers between devices with their start and end apart: 2 -> 3, of which waited for: 1 -> 2; matrix products, arithmetic and copies ran while one was open for 0% -> 0% of each run, Pallas kernels for 0% -> 2%
where the time goes in v3:
time: 57 us; the launch traced here: 56.8 us
  blocking collectives  26.3 us (46%)
  starting transfers between devices  15.9 us (28%)
  waiting for transfers between devices  7.79 us (14%)
  Pallas kernels  6.12 us (11%)
  between operations  0.69 us (1%)
    all_gather x2, blocking collectives, on_device(): pair = lax.all_gather(message, AXES, axis_index_groups=in_chip)  20.8 us
    all_to_all x1, starting transfers between devices, on_device(): lax.all_to_all(row, AXES, 0, 0, tiled=True, axis_index_groups=second_groups)  8.81 us
    all_gather x1, blocking collectives, on_device(): both = lax.all_gather(message, AXES, axis_index_groups=across_chips)  5.43 us
    all_to_all x1, starting transfers between devices, on_device(): lax.all_to_all(row, AXES, 0, 0, tiled=True, axis_index_groups=first_groups)  5.17 us
    all_to_all x1, waiting for transfers between devices, on_device(): lax.all_to_all(row, AXES, 0, 0, tiled=True, axis_index_groups=first_groups)  4.83 us
    all_to_all x1, waiting for transfers between devices, on_device(): lax.all_to_all(row, AXES, 0, 0, tiled=True, axis_index_groups=second_groups)  2.96 us
    ppermute x1, starting transfers between devices, on_device(): outer_other = lax.ppermute(outer, AXES, swap)  1.92 us
    pallas_call x1, Pallas kernels, on_device(): call(prepare, [FIELD] * 6 + [FACE, (5, *FACE), jax.ShapeDtypeStruct((1, C...  1.76 us
  transfers between devices with their start and end apart: 3, of which 2 were waited for; matrix products, arithmetic and copies ran while one was open for 0% of the time, Pallas kernels for 2%

profile of v3, /device:TPU:1, one launch (start us, length us, event | category | flops | bytes accessed | tf_op | source)
XLA Modules:
  0.0 56.8 jit_solution(15802620591544440495)
XLA Ops:
  0.6 1.8 %shard_map.59 = (f32[8,64,128]{2,1,0:T(8,128)S(1)}, f32[8,64,128]{2,1,0:T(8,128)S(1)}, f32[8,64,128]{2,1,0:T(8,128)S(1)}, f32[8,64,128]{2,1,0:T(8,128)S(1)}, f32...) custom-call(s32[1,128]{1,0:T(1,128)} %order_in.1, ...), custom_call_target="tpu_custom_call" | custom-call | flops 4000000 | bytes 2097152 | tf_op jit(solution)/shard_map/pallas_call | solution.py:478
  2.4 12.1 %all-gather = f32[10,64,128]{2,1,0:T(8,128)S(1)} all-gather(f32[5,64,128]{2,1,0:T(8,128)S(1)} %get-tuple-element.34), channel_id=2, replica_groups={{1,0},{3,2},{5,4},{7,6},{9,8},{11,10},{13,12},{15,14},{17,16},{19,18},{..., dimensions={0}, use_global_device_ids=true | all-gather | bytes 491520 | tf_op jit(solution)/shard_map/all_gather | solution.py:489
  14.6 0.6 %shard_map.60 = (f32[8,64,128]{2,1,0:T(8,128)S(1)}, f32[8,64,128]{2,1,0:T(8,128)S(1)}, f32[8,64,128]{2,1,0:T(8,128)S(1)}, f32[8,64,128]{2,1,0:T(8,128)S(1)}, f32...) custom-call(f32[8,64,128]{2,1,0:T(8,128)S(1)} %get-tuple-element.28.load, f32[8,64,128]{2,1,0:T(8,128)S(1)} %get-tuple-element.29.geo_a, ...), custom_call_target="tpu_custom_call" | custom-call | flops 4000000 | bytes 2097152 | tf_op jit(solution)/shard_map/pallas_call | solution.py:490
  15.1 5.4 %all-gather.1 = f32[10,64,128]{2,1,0:T(8,128)S(1)} all-gather(f32[5,64,128]{2,1,0:T(8,128)S(1)} %get-tuple-element.35), channel_id=3, replica_groups={{1,2},{3,4},{5,6},{7,8},{9,10},{11,12},{13,14},{15,16},{17,18},{19,20},..., dimensions={0}, use_global_device_ids=true | all-gather | bytes 491520 | tf_op jit(solution)/shard_map/all_gather | solution.py:493
  20.6 0.7 %shard_map.61 = (f32[64,128]{1,0:T(8,128)S(1)}, f32[8,64,128]{2,1,0:T(8,128)S(1)}, f32[8,64,128]{2,1,0:T(8,128)S(1)}, f32[2,64,128]{2,1,0:T(8,128)S(1)}) custom-call(f32[2,5,64,128]{3,2,1,0:T(8,128)S(1)} %bitcast.15, f32[8,64,128]{2,1,0:T(8,128)S(1)} %get-tuple-element.29.geo_a, f32[8,64,128]{2,1,0:T(8,128)S(1)} %get-tuple-element.30.geo_b, ...), custom_call_target="tpu_custom_call" | custom-call | flops 4000000 | bytes 2097152 | tf_op jit(solution)/shard_map/pallas_call | solution.py:494
  21.3 8.7 %all-gather.2 = f32[4,64,128]{2,1,0:T(8,128)S(1)} all-gather(f32[2,64,128]{2,1,0:T(8,128)S(1)} %get-tuple-element.40), channel_id=4, replica_groups={{1,0},{3,2},{5,4},{7,6},{9,8},{11,10},{13,12},{15,14},{17,16},{19,18},{..., dimensions={0}, use_global_device_ids=true | all-gather | bytes 196608 | tf_op jit(solution)/shard_map/all_gather | solution.py:500
  30.0 1.1 %shard_map.62 = (f32[64,128]{1,0:T(8,128)S(1)}, f32[8,64,128]{2,1,0:T(8,128)S(1)}, f32[64,128]{1,0:T(8,128)S(1)}, f32[24,128]{1,0:T(8,128)}) custom-call(f32[2,2,64,128]{3,2,1,0:T(8,128)S(1)} %bitcast.16, f32[4,64,128]{2,1,0:T(8,128)S(1)} %get-tuple-element.41.end, f32[8,64,128]{2,1,0:T(8,128)S(1)} %get-tuple-element.29.geo_a, ...), custom_call_target="tpu_custom_call" | custom-call | flops 4000000 | bytes 2097152 | tf_op jit(solution)/shard_map/pallas_call | solution.py:501
  31.1 5.2 %all-to-all-start = ((f32[24,1,128]{2,1,0:T(1,128)}), f32[24,1,128]{2,1,0:T(1,128)S(1)}, u32[]{:S(2)}, u32[]{:S(2)}) async-start(f32[24,1,128]{2,1,0:T(1,128)} %bitcast.7), calls=%async_computation | async-start | bytes 24576 | tf_op jit(solution)/shard_map/all_to_all | solution.py:514
  36.3 1.9 %collective-permute-start = (f32[64,128]{1,0:T(8,128)S(1)}, f32[64,128]{1,0:T(8,128)S(1)}, u32[]{:S(2)}, u32[]{:S(2)}) collective-permute-start(f32[64,128]{1,0:T(8,128)S(1)} %get-tuple-element.46.outer), channel_id=1, source_target_pairs={{0,767},{1,2},{2,1},{3,4},{4,3},{5,6},{6,5},{7,8},{8,7},{9,10},{10... | collective-permute-start | bytes 98312 | tf_op jit(solution)/shard_map/ppermute | solution.py:513
  38.2 4.8 %all-to-all-done = f32[24,1,128]{2,1,0:T(1,128)S(1)} async-done(((f32[24,1,128]{2,1,0:T(1,128)}), f32[24,1,128]{2,1,0:T(1,128)S(1)}, u32[]{:S(2)}, u32[]{:S(2)}) %all-to-all-start) | async-done | bytes 12320 | tf_op jit(solution)/shard_map/all_to_all | solution.py:514
  43.0 0.6 %shard_map.63 = f32[32,128]{1,0:T(8,128)} custom-call(f32[24,128]{1,0:T(8,128)S(1)} %bitcast.18), custom_call_target="tpu_custom_call" | custom-call | flops 100000 | bytes 2097152 | tf_op jit(solution)/shard_map/pallas_call | solution.py:515
  43.6 8.8 %all-to-all-start.1 = ((f32[32,1,128]{2,1,0:T(1,128)}), f32[32,1,128]{2,1,0:T(1,128)S(1)}, u32[]{:S(2)}, u32[]{:S(2)}) async-start(f32[32,1,128]{2,1,0:T(1,128)} %bitcast.10), calls=%async_computation.1 | async-start | bytes 32768 | tf_op jit(solution)/shard_map/all_to_all | solution.py:516
  52.5 0.3 shard_map.65
  52.7 3.0 %all-to-all-done.1 = f32[32,1,128]{2,1,0:T(1,128)S(1)} async-done(((f32[32,1,128]{2,1,0:T(1,128)}), f32[32,1,128]{2,1,0:T(1,128)S(1)}, u32[]{:S(2)}, u32[]{:S(2)}) %all-to-all-start.1) | async-done | bytes 16416 | tf_op jit(solution)/shard_map/all_to_all | solution.py:516
  55.7 0.1 shard_map.64.alpha_ref
  55.8 0.0 collective-permute-done.outer_other
  55.8 1.0 %shard_map.66 = (f32[8,8,8,128]{3,2,1,0:T(8,128)}, f32[8,8,8,128]{3,2,1,0:T(8,128)}) custom-call(f32[8,128]{1,0:T(8,128)S(1)} %shard_map.64.alpha_ref, s32[1,128]{1,0:T(1,128)S(1)} %get-tuple-element.45.order_ref, f32[64,128]{1,0:T(8,128)S(1)} %get-tuple-element.46.outer, f32[64,128]{1,0:T(8,128)S(1)} %collective-permute-done.outer_other, ...), custom_call_target="tpu_custom_call" | custom-call | flops 4000000 | bytes 2097152 | tf_op jit(solution)/shard_map/pallas_call | solution.py:519
Async XLA Ops:
  31.1 11.9 %all-to-all-start = ((f32[24,1,128]{2,1,0:T(1,128)}), f32[24,1,128]{2,1,0:T(1,128)S(1)}, u32[]{:S(2)}, u32[]{:S(2)}) async-start(f32[24,1,128]{2,1,0:T(1,128)} %bitcast.7), calls=%async_computation | async-start | bytes 24576 | tf_op jit(solution)/shard_map/all_to_all | solution.py:514
  36.3 19.5 %collective-permute-start = (f32[64,128]{1,0:T(8,128)S(1)}, f32[64,128]{1,0:T(8,128)S(1)}, u32[]{:S(2)}, u32[]{:S(2)}) collective-permute-start(f32[64,128]{1,0:T(8,128)S(1)} %get-tuple-element.46.outer), channel_id=1, source_target_pairs={{0,767},{1,2},{2,1},{3,4},{4,3},{5,6},{6,5},{7,8},{8,7},{9,10},{10... | collective-permute-start | bytes 98312 | tf_op jit(solution)/shard_map/ppermute | solution.py:513
  43.6 12.0 %all-to-all-start.1 = ((f32[32,1,128]{2,1,0:T(1,128)}), f32[32,1,128]{2,1,0:T(1,128)S(1)}, u32[]{:S(2)}, u32[]{:S(2)}) async-start(f32[32,1,128]{2,1,0:T(1,128)} %bitcast.10), calls=%async_computation.1 | async-start | bytes 32768 | tf_op jit(solution)/shard_map/all_to_all | solution.py:516

commit v4 on v3

--- a/solution.py
+++ b/solution.py
@@ -12,14 +12,23 @@
 
 TORUS = (8, 12, 4, 2)
 AXES = ("ty", "tz", "tx", "core")
-ROOT = (5, 10, 3, 1)
+LINE_ROOT = (10, 10, 10, 9)
+PLANE_ROOT = (5, 3)
 
 
 def groups(axes):
     ids = np.arange(np.prod(TORUS)).reshape(TORUS)
-    ids = np.roll(ids, [-r for r in ROOT], range(4))
-    others = [d for d in range(4) if d not in axes]
-    return ids.transpose(*others, *axes).reshape(-1, np.prod([TORUS[d] for d in axes])).tolist()
+    out = []
+    if axes == (1, 3):
+        for y in range(TORUS[0]):
+            for x in range(TORUS[2]):
+                z = LINE_ROOT[x]
+                out.append(np.roll(ids[y, :, x, :], [-z, -1], (0, 1)).reshape(-1).tolist())
+        return out
+    for z in range(TORUS[1]):
+        for c in range(TORUS[3]):
+            out.append(np.roll(ids[:, z, :, c], [-PLANE_ROOT[0], -PLANE_ROOT[1]], (0, 1)).reshape(-1).tolist())
+    return out
 
 
 NODES = 8
@@ -140,6 +149,8 @@
         self.has_high = lane < CELLS - EL_Z
         self.first = row == 0
         self.last = row == NODES - 1
+        self.front = pos_z == 0
+        self.back = pos_z == EL_Z - 1
 
     def plane(self, rows):
         low, high = rows[0], rows[-1]
@@ -156,6 +167,20 @@
         return out
 
 
+def share(shared, ref, a, rows):
+    low, high = rows[0], rows[-1]
+    zero = jnp.zeros_like(low)
+    new_low = low + jnp.where(shared.has_low, pltpu.roll(high, EL_Z, 1), zero)
+    new_high = high + jnp.where(shared.has_high, pltpu.roll(low, CELLS - EL_Z, 1), zero)
+    put_rows(ref, [new_low, *rows[1:-1], new_high], a)
+    near, far = pl.ds(0, NODES, stride=8), pl.ds(NODES - 1, NODES, stride=8)
+    first, last = ref[a, near, :], ref[a, far, :]
+    before = jnp.where(shared.front, pltpu.roll(last, CELLS - EL_Z + 1, 1), pltpu.roll(last, 1, 1))
+    after = jnp.where(shared.back, pltpu.roll(first, EL_Z - 1, 1), pltpu.roll(first, CELLS - 1, 1))
+    ref[a, near, :] = first + before
+    ref[a, far, :] = last + after
+
+
 def rows_of(ref, *at):
     return [ref[(*at, pl.ds(8 * b, 8), slice(None))] for b in range(NODES)]
 
@@ -192,7 +217,7 @@
         index_ref[...] = index.astype(jnp.int32)
 
     at = mirrored()
-    for copy in copies:
+    for copy in copies[:3]:
         copy.wait()
     index = index_ref[...]
 
@@ -216,6 +241,8 @@
             put_rows(work, square_back(lines), a)
         elif a == NODES - 1:
             put_rows(message, lines, 4)
+    for copy in copies[3:]:
+        copy.wait()
     for a in range(NODES):
         lines, weights, values = fetch(1, a), fetch(3, a), fetch(4, a)
         put_rows(geo_b, lines, a)
@@ -261,11 +288,12 @@
     put_rows(end, lead_7, 0)
     put_rows(end, fac_b, 1)
     put_rows(end, fac_c, 2)
-    put_rows(end, within(tail, mass_7, fac_b, fac_c, keep, work), 3)
+    put_rows(end, mass_7, 3)
     for a in range(1, NODES - 1):
-        top, low = shared.plane(rows_of(load, a)), shared.plane(rows_of(diag, a))
-        low = [1.0 / v for v in low]
-        put_rows(start, top, a)
+        share(shared, start, a, rows_of(load, a))
+        share(shared, recip, a, rows_of(diag, a))
+    for a in range(1, NODES - 1):
+        top, low = rows_of(start, a), [1.0 / v for v in rows_of(recip, a)]
         put_rows(recip, low, a)
         put_rows(first, [x * y * F32(1.0 / CENTRE) for x, y in zip(top, low)], a)
     for b in range(NODES):
@@ -281,13 +309,19 @@
     put_rows(message, rows_of(geo_b, 0), 3)
     put_rows(message, rows_of(geo_c, 0), 4)
 
+    @pl.when(lax.axis_index("core") == 0)
+    def inner():
+        tail = rows_of(first, NODES - 1)
+        put_rows(end, within(tail, rows_of(end, 3), rows_of(end, 1), rows_of(end, 2), keep, work), 3)
+
 
 def improve(first, image, recip):
     return [u * F32(KEEP) + q * d * F32(PULL) for u, q, d in zip(first, image, recip)]
 
 
-def middle(both, geo_a, geo_b, geo_c, mass, recip, first, slope, start0, precond, ahead, message, keep, local, work):
+def middle(both, end, geo_a, geo_b, geo_c, mass, recip, first, slope, start0, precond, ahead, message, keep, local, work):
     shared = Shared()
+    once = (1 - lax.axis_index("core")).astype(F32)
     lead, fac_b, fac_c = summed(both, 2), summed(both, 3), summed(both, 4)
     top, low, head = settle(shared, summed(both, 0), lead, fac_b, fac_c, work.at[0])
     put_rows(start0, top)
@@ -302,7 +336,7 @@
         back = derive_back(flux)
         for a in range(1, NODES - 1):
             local[a, here, :] = back[a]
-        message[0, here, :] = back[NODES - 1]
+        message[0, here, :] = back[NODES - 1] + end[3, here, :] * once
     for a in range(1, NODES - 1):
         put_rows(work, stiff_line(turned(first, a), rows_of(geo_c, a)), a)
     for a in range(1, NODES - 1):
@@ -326,7 +360,7 @@
 
 def finish(pair, end, geo_a, geo_b, geo_c, mass, load, recip, first, precond_in, ahead, precond, image, outer, row, keep, flux_a, flux_b, flux_c, row_buf, row_sem):
     shared = Shared()
-    whole = shared.plane([x + y for x, y in zip(summed(pair, 0), rows_of(end, 3))])
+    whole = shared.plane(summed(pair, 0))
     tail = improve(rows_of(first, NODES - 1), whole, rows_of(recip, NODES - 1))
     put_rows(precond, tail)
 
@@ -382,7 +416,7 @@
                 for x, y, z, m, v in zip(rows_of(flux_a, a), part, turn, rows_of(mass, a), values)
             ]
             if a == 0:
-                put_rows(outer, total)
+                put_rows(outer, Shared().plane(total))
             else:
                 put_rows(image, Shared().plane(total), a)
         inside = within(rows_of(precond), rows_of(end, 0), rows_of(end, 1), rows_of(end, 2), keep, flux_c.at[NODES - 1])
@@ -392,16 +426,15 @@
     row_copy.wait()
 
 
-def restore(order_ref, start_in, start0, precond_in, last, image_in, start, precond, image):
+def restore(order_ref, start_in, start0, precond_in, last, image_in, outer, start, precond, image):
     index = jnp.broadcast_to(order_ref[...], (8, CELLS))
     for a in range(NODES):
         for out, rows in (
             (start, rows_of(start0) if a == 0 else rows_of(start_in, a)),
             (precond, rows_of(last) if a == NODES - 1 else rows_of(precond_in, a)),
-            (image, None if a == 0 else rows_of(image_in, a)),
+            (image, rows_of(outer) if a == 0 else rows_of(image_in, a)),
         ):
-            if rows is not None:
-                put_rows(out, [lanes_of(v, index) for v in rows], a)
+            put_rows(out, [lanes_of(v, index) for v in rows], a)
 
 
 def step_length(sums, alpha):
@@ -413,23 +446,28 @@
     alpha[...] = jnp.broadcast_to(over / under, (8, 128))
 
 
-def close(alpha_ref, order_ref, outer, outer_other, start, precond, image, solution_out, residual_out, buf_s, buf_r, sems):
-    shared = Shared()
+def close(alpha_ref, order_ref, other, start, precond, image, solution_out, residual_out, buf_s, buf_r, sems):
     alpha = alpha_ref[...]
     index = jnp.broadcast_to(order_ref[...], (8, CELLS))
     at = mirrored()
-    head = shared.plane([x + y for x, y in zip(rows_of(outer), rows_of(outer_other))])
-    head = [lanes_of(v, index) for v in head]
+    other = [lanes_of(v, index) for v in rows_of(other)]
     copies = []
+
+    def send(i, a):
+        buf, out = ((buf_s, solution_out), (buf_r, residual_out))[i]
+        copies.append(pltpu.make_async_copy(buf.at[a], out.at[at[a]], sems.at[i, a]))
+        copies[-1].start()
+
     for a in (1, 2, 3, 4, 5, 6, 7, 0):
-        rows = head if a == 0 else rows_of(image, a)
-        for b, (v, s, i) in enumerate(zip(rows_of(precond, a), rows_of(start, a), rows)):
+        for b, v in enumerate(rows_of(precond, a)):
             buf_s[a, b] = alpha * v
+        send(0, a)
+        rows = rows_of(image, a)
+        if a == 0:
+            rows = [x + y for x, y in zip(rows, other)]
+        for b, (s, i) in enumerate(zip(rows_of(start, a), rows)):
             buf_r[a, b] = s - alpha * i
-        for i, (buf, out) in enumerate(((buf_s, solution_out), (buf_r, residual_out))):
-            copy = pltpu.make_async_copy(buf.at[a], out.at[at[a]], sems.at[i, a])
-            copy.start()
-            copies.append(copy)
+        send(1, a)
     for copy in copies:
         copy.wait()
 
@@ -494,9 +532,9 @@
     start0, precond, ahead, message = call(
         middle,
         [FACE, FIELD, FIELD, (2, *FACE)],
-        [VMEM] * 8,
+        [VMEM] * 9,
         [pltpu.VMEM(FACE, F32), pltpu.VMEM(FIELD, F32), pltpu.VMEM(FIELD, F32)],
-    )(both, geo_a, geo_b, geo_c, mass, recip, first, slope)
+    )(both, end, geo_a, geo_b, geo_c, mass, recip, first, slope)
     pair = lax.all_gather(message, AXES, axis_index_groups=in_chip)
     last, image, outer, row = call(
         finish,
@@ -515,14 +553,14 @@
     (row,) = call(gather_up, [(len(second_groups[0]), 128)], [VMEM], flops=100_000)(sums)
     sums = lax.all_to_all(row, AXES, 0, 0, tiled=True, axis_index_groups=second_groups)
     (alpha,) = call(step_length, [(8, 128)], [VMEM], flops=100_000)(sums)
-    start, precond, image = call(restore, [FIELD] * 3, [VMEM] * 6)(order, start, start0, precond, last, image)
+    start, precond, image = call(restore, [FIELD] * 3, [VMEM] * 7)(order, start, start0, precond, last, image, outer)
     solution, residual = call(
         close,
         [BLOCK, BLOCK],
-        [VMEM] * 7,
+        [VMEM] * 6,
         [pltpu.VMEM(BLOCK, F32), pltpu.VMEM(BLOCK, F32), dma((2, NODES))],
         out_specs=[ANY, ANY],
-    )(alpha, order, outer, outer_other, start, precond, image)
+    )(alpha, order, outer_other, start, precond, image)
     return solution, residual
 
 

time: 57 us -> 56.6 us (level)
  no operation moved by 1% of the time
where the time goes in v4:
time: 56.6 us; the launch traced here: 56.3 us
  blocking collectives  26.3 us (46%)
  starting transfers between devices  15.9 us (28%)
  waiting for transfers between devices  7.78 us (14%)
  Pallas kernels  5.75 us (10%)
  between operations  0.69 us (1%)
    all_gather x2, blocking collectives, on_device(): pair = lax.all_gather(message, AXES, axis_index_groups=in_chip)  20.8 us
    all_to_all x1, starting transfers between devices, on_device(): lax.all_to_all(row, AXES, 0, 0, tiled=True, axis_index_groups=second_groups)  8.77 us
    all_gather x1, blocking collectives, on_device(): both = lax.all_gather(message, AXES, axis_index_groups=across_chips)  5.43 us
    all_to_all x1, starting transfers between devices, on_device(): lax.all_to_all(row, AXES, 0, 0, tiled=True, axis_index_groups=first_groups)  5.17 us
    all_to_all x1, waiting for transfers between devices, on_device(): lax.all_to_all(row, AXES, 0, 0, tiled=True, axis_index_groups=first_groups)  4.83 us
    all_to_all x1, waiting for transfers between devices, on_device(): lax.all_to_all(row, AXES, 0, 0, tiled=True, axis_index_groups=second_groups)  2.95 us
    ppermute x1, starting transfers between devices, on_device(): outer_other = lax.ppermute(outer, AXES, swap)  1.92 us
    pallas_call x1, Pallas kernels, on_device(): call(prepare, [FIELD] * 6 + [FACE, (5, *FACE), jax.ShapeDtypeStruct((1, C...  1.69 us
  transfers between devices with their start and end apart: 3, of which 2 were waited for; matrix products, arithmetic and copies ran while one was open for 0% of the time, Pallas kernels for 2%

profile of v4, /device:TPU:1, one launch (start us, length us, event | category | flops | bytes accessed | tf_op | source)
XLA Modules:
  0.0 56.3 jit_solution(8197010225695119123)
XLA Ops:
  0.6 1.7 %shard_map.59 = (f32[8,64,128]{2,1,0:T(8,128)S(1)}, f32[8,64,128]{2,1,0:T(8,128)S(1)}, f32[8,64,128]{2,1,0:T(8,128)S(1)}, f32[8,64,128]{2,1,0:T(8,128)S(1)}, f32...) custom-call(s32[1,128]{1,0:T(1,128)} %order_in.1, ...), custom_call_target="tpu_custom_call" | custom-call | flops 4000000 | bytes 2097152 | tf_op jit(solution)/shard_map/pallas_call | solution.py:516
  2.3 12.1 %all-gather = f32[10,64,128]{2,1,0:T(8,128)S(1)} all-gather(f32[5,64,128]{2,1,0:T(8,128)S(1)} %get-tuple-element.34), channel_id=2, replica_groups={{1,0},{3,2},{5,4},{7,6},{9,8},{11,10},{13,12},{15,14},{17,16},{19,18},{..., dimensions={0}, use_global_device_ids=true | all-gather | bytes 491520 | tf_op jit(solution)/shard_map/all_gather | solution.py:527
  14.5 0.4 shard_map.60
  14.8 5.4 %all-gather.1 = f32[10,64,128]{2,1,0:T(8,128)S(1)} all-gather(f32[5,64,128]{2,1,0:T(8,128)S(1)} %get-tuple-element.35), channel_id=3, replica_groups={{1,2},{3,4},{5,6},{7,8},{9,10},{11,12},{13,14},{15,16},{17,18},{19,20},..., dimensions={0}, use_global_device_ids=true | all-gather | bytes 491520 | tf_op jit(solution)/shard_map/all_gather | solution.py:531
  20.3 0.7 %shard_map.61 = (f32[64,128]{1,0:T(8,128)S(1)}, f32[8,64,128]{2,1,0:T(8,128)S(1)}, f32[8,64,128]{2,1,0:T(8,128)S(1)}, f32[2,64,128]{2,1,0:T(8,128)S(1)}) custom-call(f32[2,5,64,128]{3,2,1,0:T(8,128)S(1)} %bitcast.15, f32[4,64,128]{2,1,0:T(8,128)S(1)} %get-tuple-element.36.end, f32[8,64,128]{2,1,0:T(8,128)S(1)} %get-tuple-element.29.geo_a, ...), custom_call_target="tpu_custom_call" | custom-call | flops 4000000 | bytes 2097152 | tf_op jit(solution)/shard_map/pallas_call | solution.py:532
  21.0 8.7 %all-gather.2 = f32[4,64,128]{2,1,0:T(8,128)S(1)} all-gather(f32[2,64,128]{2,1,0:T(8,128)S(1)} %get-tuple-element.41), channel_id=4, replica_groups={{1,0},{3,2},{5,4},{7,6},{9,8},{11,10},{13,12},{15,14},{17,16},{19,18},{..., dimensions={0}, use_global_device_ids=true | all-gather | bytes 196608 | tf_op jit(solution)/shard_map/all_gather | solution.py:538
  29.7 1.1 %shard_map.62 = (f32[64,128]{1,0:T(8,128)S(1)}, f32[8,64,128]{2,1,0:T(8,128)S(1)}, f32[64,128]{1,0:T(8,128)S(1)}, f32[24,128]{1,0:T(8,128)}) custom-call(f32[2,2,64,128]{3,2,1,0:T(8,128)S(1)} %bitcast.16, f32[4,64,128]{2,1,0:T(8,128)S(1)} %get-tuple-element.36.end, f32[8,64,128]{2,1,0:T(8,128)S(1)} %get-tuple-element.29.geo_a, ...), custom_call_target="tpu_custom_call" | custom-call | flops 4000000 | bytes 2097152 | tf_op jit(solution)/shard_map/pallas_call | solution.py:539
  30.8 5.2 %all-to-all-start = ((f32[24,1,128]{2,1,0:T(1,128)}), f32[24,1,128]{2,1,0:T(1,128)S(1)}, u32[]{:S(2)}, u32[]{:S(2)}) async-start(f32[24,1,128]{2,1,0:T(1,128)} %bitcast.7), calls=%async_computation | async-start | bytes 24576 | tf_op jit(solution)/shard_map/all_to_all | solution.py:552
  36.0 1.9 %collective-permute-start = (f32[64,128]{1,0:T(8,128)S(1)}, f32[64,128]{1,0:T(8,128)S(1)}, u32[]{:S(2)}, u32[]{:S(2)}) collective-permute-start(f32[64,128]{1,0:T(8,128)S(1)} %get-tuple-element.46.outer), channel_id=1, source_target_pairs={{0,767},{1,2},{2,1},{3,4},{4,3},{5,6},{6,5},{7,8},{8,7},{9,10},{10... | collective-permute-start | bytes 98312 | tf_op jit(solution)/shard_map/ppermute | solution.py:551
  37.9 4.8 %all-to-all-done = f32[24,1,128]{2,1,0:T(1,128)S(1)} async-done(((f32[24,1,128]{2,1,0:T(1,128)}), f32[24,1,128]{2,1,0:T(1,128)S(1)}, u32[]{:S(2)}, u32[]{:S(2)}) %all-to-all-start) | async-done | bytes 12320 | tf_op jit(solution)/shard_map/all_to_all | solution.py:552
  42.7 0.6 %shard_map.63 = f32[32,128]{1,0:T(8,128)} custom-call(f32[24,128]{1,0:T(8,128)S(1)} %bitcast.18), custom_call_target="tpu_custom_call" | custom-call | flops 100000 | bytes 2097152 | tf_op jit(solution)/shard_map/pallas_call | solution.py:553
  43.3 8.8 %all-to-all-start.1 = ((f32[32,1,128]{2,1,0:T(1,128)}), f32[32,1,128]{2,1,0:T(1,128)S(1)}, u32[]{:S(2)}, u32[]{:S(2)}) async-start(f32[32,1,128]{2,1,0:T(1,128)} %bitcast.10), calls=%async_computation.1 | async-start | bytes 32768 | tf_op jit(solution)/shard_map/all_to_all | solution.py:554
  52.1 0.3 shard_map.65
  52.4 2.9 %all-to-all-done.1 = f32[32,1,128]{2,1,0:T(1,128)S(1)} async-done(((f32[32,1,128]{2,1,0:T(1,128)}), f32[32,1,128]{2,1,0:T(1,128)S(1)}, u32[]{:S(2)}, u32[]{:S(2)}) %all-to-all-start.1) | async-done | bytes 16416 | tf_op jit(solution)/shard_map/all_to_all | solution.py:554
  55.3 0.1 shard_map.64.alpha_ref
  55.4 0.0 collective-permute-done.other
  55.4 0.9 %shard_map.66 = (f32[8,8,8,128]{3,2,1,0:T(8,128)}, f32[8,8,8,128]{3,2,1,0:T(8,128)}) custom-call(f32[8,128]{1,0:T(8,128)S(1)} %shard_map.64.alpha_ref, s32[1,128]{1,0:T(1,128)S(1)} %get-tuple-element.45.order_ref, f32[64,128]{1,0:T(8,128)S(1)} %collective-permute-done.other, f32[8,64,128]{2,1,0:T(8,128)S(1)} %get-tuple-element.51.start, ...), custom_call_target="tpu_custom_call" | custom-call | flops 4000000 | bytes 2097152 | tf_op jit(solution)/shard_map/pallas_call | solution.py:557
Async XLA Ops:
  30.8 11.9 %all-to-all-start = ((f32[24,1,128]{2,1,0:T(1,128)}), f32[24,1,128]{2,1,0:T(1,128)S(1)}, u32[]{:S(2)}, u32[]{:S(2)}) async-start(f32[24,1,128]{2,1,0:T(1,128)} %bitcast.7), calls=%async_computation | async-start | bytes 24576 | tf_op jit(solution)/shard_map/all_to_all | solution.py:552
  36.0 19.5 %collective-permute-start = (f32[64,128]{1,0:T(8,128)S(1)}, f32[64,128]{1,0:T(8,128)S(1)}, u32[]{:S(2)}, u32[]{:S(2)}) collective-permute-start(f32[64,128]{1,0:T(8,128)S(1)} %get-tuple-element.46.outer), channel_id=1, source_target_pairs={{0,767},{1,2},{2,1},{3,4},{4,3},{5,6},{6,5},{7,8},{8,7},{9,10},{10... | collective-permute-start | bytes 98312 | tf_op jit(solution)/shard_map/ppermute | solution.py:551
  43.3 12.0 %all-to-all-start.1 = ((f32[32,1,128]{2,1,0:T(1,128)}), f32[32,1,128]{2,1,0:T(1,128)S(1)}, u32[]{:S(2)}, u32[]{:S(2)}) async-start(f32[32,1,128]{2,1,0:T(1,128)} %bitcast.10), calls=%async_computation.1 | async-start | bytes 32768 | tf_op jit(solution)/shard_map/all_to_all | solution.py:554

commit v5 on v4

--- a/solution.py
+++ b/solution.py
@@ -104,7 +104,8 @@
 
 def derive(values):
     even, odd = fold(values)
-    by_even = [combine(ON_SUM[m], even) for m in range(HALF_N)]
+    even = [v - even[-1] for v in even[:-1]]
+    by_even = [combine(ON_SUM[m, :-1], even) for m in range(HALF_N)]
     by_odd = [combine(ON_DIFF[m], odd) for m in range(HALF_N)]
     return [a + b for a, b in zip(by_even, by_odd)] + [
         b - a for a, b in zip(by_even[::-1], by_odd[::-1])
@@ -114,7 +115,8 @@
 def derive_back(values):
     even, odd = fold(values)
     by_even = [combine(ON_DIFF[:, a], even) for a in range(HALF_N)]
-    by_odd = [combine(ON_SUM[:, a], odd) for a in range(HALF_N)]
+    by_odd = [combine(ON_SUM[:, a], odd) for a in range(HALF_N - 1)]
+    by_odd.append(-(by_odd[0] + by_odd[1] + by_odd[2]))
     return [a + b for a, b in zip(by_even, by_odd)] + [
         b - a for a, b in zip(by_even[::-1], by_odd[::-1])
     ]

time: 56.6 us -> 56.6 us (level)
  no operation moved by 1% of the time
where the time goes in v5:
time: 56.6 us; the launch traced here: 56.3 us
  blocking collectives  26.3 us (46%)
  starting transfers between devices  15.9 us (28%)
  waiting for transfers between devices  7.78 us (14%)
  Pallas kernels  5.72 us (10%)
  between operations  0.69 us (1%)
    all_gather x2, blocking collectives, on_device(): pair = lax.all_gather(message, AXES, axis_index_groups=in_chip)  20.8 us
    all_to_all x1, starting transfers between devices, on_device(): lax.all_to_all(row, AXES, 0, 0, tiled=True, axis_index_groups=second_groups)  8.77 us
    all_gather x1, blocking collectives, on_device(): both = lax.all_gather(message, AXES, axis_index_groups=across_chips)  5.43 us
    all_to_all x1, starting transfers between devices, on_device(): lax.all_to_all(row, AXES, 0, 0, tiled=True, axis_index_groups=first_groups)  5.17 us
    all_to_all x1, waiting for transfers between devices, on_device(): lax.all_to_all(row, AXES, 0, 0, tiled=True, axis_index_groups=first_groups)  4.83 us
    all_to_all x1, waiting for transfers between devices, on_device(): lax.all_to_all(row, AXES, 0, 0, tiled=True, axis_index_groups=second_groups)  2.95 us
    ppermute x1, starting transfers between devices, on_device(): outer_other = lax.ppermute(outer, AXES, swap)  1.92 us
    pallas_call x1, Pallas kernels, on_device(): call(prepare, [FIELD] * 6 + [FACE, (5, *FACE), jax.ShapeDtypeStruct((1, C...  1.69 us
  transfers between devices with their start and end apart: 3, of which 2 were waited for; matrix products, arithmetic and copies ran while one was open for 0% of the time, Pallas kernels for 2%

profile of v5, /device:TPU:1, one launch (start us, length us, event | category | flops | bytes accessed | tf_op | source)
XLA Modules:
  0.0 56.3 jit_solution(4855592663269087605)
XLA Ops:
  0.6 1.7 %shard_map.59 = (f32[8,64,128]{2,1,0:T(8,128)S(1)}, f32[8,64,128]{2,1,0:T(8,128)S(1)}, f32[8,64,128]{2,1,0:T(8,128)S(1)}, f32[8,64,128]{2,1,0:T(8,128)S(1)}, f32...) custom-call(s32[1,128]{1,0:T(1,128)} %order_in.1, ...), custom_call_target="tpu_custom_call" | custom-call | flops 4000000 | bytes 2097152 | tf_op jit(solution)/shard_map/pallas_call | solution.py:518
  2.3 12.1 %all-gather = f32[10,64,128]{2,1,0:T(8,128)S(1)} all-gather(f32[5,64,128]{2,1,0:T(8,128)S(1)} %get-tuple-element.34), channel_id=2, replica_groups={{1,0},{3,2},{5,4},{7,6},{9,8},{11,10},{13,12},{15,14},{17,16},{19,18},{..., dimensions={0}, use_global_device_ids=true | all-gather | bytes 491520 | tf_op jit(solution)/shard_map/all_gather | solution.py:529
  14.5 0.3 shard_map.60
  14.8 5.4 %all-gather.1 = f32[10,64,128]{2,1,0:T(8,128)S(1)} all-gather(f32[5,64,128]{2,1,0:T(8,128)S(1)} %get-tuple-element.35), channel_id=3, replica_groups={{1,2},{3,4},{5,6},{7,8},{9,10},{11,12},{13,14},{15,16},{17,18},{19,20},..., dimensions={0}, use_global_device_ids=true | all-gather | bytes 491520 | tf_op jit(solution)/shard_map/all_gather | solution.py:533
  20.3 0.7 %shard_map.61 = (f32[64,128]{1,0:T(8,128)S(1)}, f32[8,64,128]{2,1,0:T(8,128)S(1)}, f32[8,64,128]{2,1,0:T(8,128)S(1)}, f32[2,64,128]{2,1,0:T(8,128)S(1)}) custom-call(f32[2,5,64,128]{3,2,1,0:T(8,128)S(1)} %bitcast.15, f32[4,64,128]{2,1,0:T(8,128)S(1)} %get-tuple-element.36.end, f32[8,64,128]{2,1,0:T(8,128)S(1)} %get-tuple-element.29.geo_a, ...), custom_call_target="tpu_custom_call" | custom-call | flops 4000000 | bytes 2097152 | tf_op jit(solution)/shard_map/pallas_call | solution.py:534
  21.0 8.7 %all-gather.2 = f32[4,64,128]{2,1,0:T(8,128)S(1)} all-gather(f32[2,64,128]{2,1,0:T(8,128)S(1)} %get-tuple-element.41), channel_id=4, replica_groups={{1,0},{3,2},{5,4},{7,6},{9,8},{11,10},{13,12},{15,14},{17,16},{19,18},{..., dimensions={0}, use_global_device_ids=true | all-gather | bytes 196608 | tf_op jit(solution)/shard_map/all_gather | solution.py:540
  29.7 1.1 %shard_map.62 = (f32[64,128]{1,0:T(8,128)S(1)}, f32[8,64,128]{2,1,0:T(8,128)S(1)}, f32[64,128]{1,0:T(8,128)S(1)}, f32[24,128]{1,0:T(8,128)}) custom-call(f32[2,2,64,128]{3,2,1,0:T(8,128)S(1)} %bitcast.16, f32[4,64,128]{2,1,0:T(8,128)S(1)} %get-tuple-element.36.end, f32[8,64,128]{2,1,0:T(8,128)S(1)} %get-tuple-element.29.geo_a, ...), custom_call_target="tpu_custom_call" | custom-call | flops 4000000 | bytes 2097152 | tf_op jit(solution)/shard_map/pallas_call | solution.py:541
  30.7 5.2 %all-to-all-start = ((f32[24,1,128]{2,1,0:T(1,128)}), f32[24,1,128]{2,1,0:T(1,128)S(1)}, u32[]{:S(2)}, u32[]{:S(2)}) async-start(f32[24,1,128]{2,1,0:T(1,128)} %bitcast.7), calls=%async_computation | async-start | bytes 24576 | tf_op jit(solution)/shard_map/all_to_all | solution.py:554
  35.9 1.9 %collective-permute-start = (f32[64,128]{1,0:T(8,128)S(1)}, f32[64,128]{1,0:T(8,128)S(1)}, u32[]{:S(2)}, u32[]{:S(2)}) collective-permute-start(f32[64,128]{1,0:T(8,128)S(1)} %get-tuple-element.46.outer), channel_id=1, source_target_pairs={{0,767},{1,2},{2,1},{3,4},{4,3},{5,6},{6,5},{7,8},{8,7},{9,10},{10... | collective-permute-start | bytes 98312 | tf_op jit(solution)/shard_map/ppermute | solution.py:553
  37.9 4.8 %all-to-all-done = f32[24,1,128]{2,1,0:T(1,128)S(1)} async-done(((f32[24,1,128]{2,1,0:T(1,128)}), f32[24,1,128]{2,1,0:T(1,128)S(1)}, u32[]{:S(2)}, u32[]{:S(2)}) %all-to-all-start) | async-done | bytes 12320 | tf_op jit(solution)/shard_map/all_to_all | solution.py:554
  42.7 0.6 %shard_map.63 = f32[32,128]{1,0:T(8,128)} custom-call(f32[24,128]{1,0:T(8,128)S(1)} %bitcast.18), custom_call_target="tpu_custom_call" | custom-call | flops 100000 | bytes 2097152 | tf_op jit(solution)/shard_map/pallas_call | solution.py:555
  43.3 8.8 %all-to-all-start.1 = ((f32[32,1,128]{2,1,0:T(1,128)}), f32[32,1,128]{2,1,0:T(1,128)S(1)}, u32[]{:S(2)}, u32[]{:S(2)}) async-start(f32[32,1,128]{2,1,0:T(1,128)} %bitcast.10), calls=%async_computation.1 | async-start | bytes 32768 | tf_op jit(solution)/shard_map/all_to_all | solution.py:556
  52.1 0.3 shard_map.65
  52.3 2.9 %all-to-all-done.1 = f32[32,1,128]{2,1,0:T(1,128)S(1)} async-done(((f32[32,1,128]{2,1,0:T(1,128)}), f32[32,1,128]{2,1,0:T(1,128)S(1)}, u32[]{:S(2)}, u32[]{:S(2)}) %all-to-all-start.1) | async-done | bytes 16416 | tf_op jit(solution)/shard_map/all_to_all | solution.py:556
  55.3 0.1 shard_map.64.alpha_ref
  55.4 0.0 collective-permute-done.other
  55.4 0.9 %shard_map.66 = (f32[8,8,8,128]{3,2,1,0:T(8,128)}, f32[8,8,8,128]{3,2,1,0:T(8,128)}) custom-call(f32[8,128]{1,0:T(8,128)S(1)} %shard_map.64.alpha_ref, s32[1,128]{1,0:T(1,128)S(1)} %get-tuple-element.45.order_ref, f32[64,128]{1,0:T(8,128)S(1)} %collective-permute-done.other, f32[8,64,128]{2,1,0:T(8,128)S(1)} %get-tuple-element.51.start, ...), custom_call_target="tpu_custom_call" | custom-call | flops 4000000 | bytes 2097152 | tf_op jit(solution)/shard_map/pallas_call | solution.py:559
Async XLA Ops:
  30.7 11.9 %all-to-all-start = ((f32[24,1,128]{2,1,0:T(1,128)}), f32[24,1,128]{2,1,0:T(1,128)S(1)}, u32[]{:S(2)}, u32[]{:S(2)}) async-start(f32[24,1,128]{2,1,0:T(1,128)} %bitcast.7), calls=%async_computation | async-start | bytes 24576 | tf_op jit(solution)/shard_map/all_to_all | solution.py:554
  35.9 19.5 %collective-permute-start = (f32[64,128]{1,0:T(8,128)S(1)}, f32[64,128]{1,0:T(8,128)S(1)}, u32[]{:S(2)}, u32[]{:S(2)}) collective-permute-start(f32[64,128]{1,0:T(8,128)S(1)} %get-tuple-element.46.outer), channel_id=1, source_target_pairs={{0,767},{1,2},{2,1},{3,4},{4,3},{5,6},{6,5},{7,8},{8,7},{9,10},{10... | collective-permute-start | bytes 98312 | tf_op jit(solution)/shard_map/ppermute | solution.py:553
  43.3 12.0 %all-to-all-start.1 = ((f32[32,1,128]{2,1,0:T(1,128)}), f32[32,1,128]{2,1,0:T(1,128)S(1)}, u32[]{:S(2)}, u32[]{:S(2)}) async-start(f32[32,1,128]{2,1,0:T(1,128)} %bitcast.10), calls=%async_computation.1 | async-start | bytes 32768 | tf_op jit(solution)/shard_map/all_to_all | solution.py:556
